TPU v7x, 32 devices: a whole 2x2x4 slice. The times are simulated.
32 devices in a mesh: dp: 8 (over z, y), tensor: 4 (over x, core).
Axes of the slice: x: 2, y: 2, z: 4, core: 2. Of those that a mesh axis runs over, the one named last changes fastest.
Arguments:
- frames: bfloat16 [8192, 1024], P(('dp', 'tensor')), may hold values from -6 to 6
- cotangent: bfloat16 [8192, 1024], P(('dp', 'tensor')), may hold values from -6 to 6
- ada_gain: float32 [7, 2048], replicated, may hold values from 0.25 to 1.75
- ada_shift: float32 [7, 2048], replicated, may hold values from -4 to 4
- w_query: bfloat16 [1024, 1024], P(None, 'tensor'), may hold values from -0.25 to 0.25
- b_query: float32 [1024], P('tensor'), may hold values from -4 to 4
- w_key: bfloat16 [1024, 1024], P(None, 'tensor'), may hold values from -0.25 to 0.25
- w_value: bfloat16 [1024, 1024], P(None, 'tensor'), may hold values from -0.1875 to 0.1875
- b_value: float32 [1024], P('tensor'), may hold values from -4 to 4
- w_out: bfloat16 [1024, 1024], P('tensor'), may hold values from -1.5 to 1.5
- b_out: float32 [1024], replicated, may hold values from -4 to 4
- w_inner: bfloat16 [1024, 4096], P(None, 'tensor'), may hold values from -0.1875 to 0.1875
- b_inner: float32 [4096], P('tensor'), may hold values from -6 to 6
- w_outer: bfloat16 [4096, 1024], P('tensor'), may hold values from -0.09375 to 0.09375
- b_outer: float32 [1024], replicated, may hold values from -6 to 6
- section_index: int32 [8], P('dp'), may hold values from 2 to 8, as said below
- lengths: int32 [8], P('dp'), may hold values from 512 to 1024, as said below
- key_mask: int32 [8192], P('dp'), may hold values from 0 to 1, as said below
Outputs:
- layer_out: bfloat16 [8192, 1024], P(('dp', 'tensor'))
- frames_grad: float32 [8192, 1024], P(('dp', 'tensor'))
- grad_ada_gain: float32 [7, 2048], replicated
- grad_ada_shift: float32 [7, 2048], replicated
- grad_w_query: float32 [1024, 1024], P(None, 'tensor')
- grad_b_query: float32 [1024], P('tensor')
- grad_w_key: float32 [1024, 1024], P(None, 'tensor')
- grad_w_value: float32 [1024, 1024], P(None, 'tensor')
- grad_b_value: float32 [1024], P('tensor')
- grad_w_out: float32 [1024, 1024], P('tensor')
- grad_b_out: float32 [1024], replicated
- grad_w_inner: float32 [1024, 4096], P(None, 'tensor')
- grad_b_inner: float32 [4096], P('tensor')
- grad_w_outer: float32 [4096, 1024], P('tensor')
- grad_b_outer: float32 [1024], replicated
Inputs may be any that keep to these rules, and one draw needn't show every extreme that they name: `section_index`: every one of the 7 sections is used by some sequence. `lengths`: some sequence has all 1024 frames. `key_mask`: the first frame of every sequence is 1.
All inputs are finite; a program needn't handle non-finite values.
Results may differ from a plain program's by a relative error of at most 0.015.
The roundings to bfloat16 on the way count: a program that leaves them out, or rounds other values in their place, can miss the bound.
Values may be sent and summed in bfloat16 or wider, within the bound.
A program may use at most 128 MiB of HBM per device.

v0:
```python
import jax
import jax.numpy as jnp
from jax import lax
from jax.sharding import PartitionSpec as P

HDIM = 64
SEQ = 1024


EPSILON = 1e-05
NEG_LARGE = -1e30
PRECISE = lax.Precision.HIGHEST


def normalize(row_block):
    centered = row_block - jnp.mean(row_block, axis=-1, keepdims=True)
    inverse = lax.rsqrt(jnp.mean(centered * centered, axis=-1, keepdims=True) + EPSILON)
    return (centered * inverse, inverse)


def norm_back(grad_hat, normed, inverse):
    return inverse * (
        grad_hat
        - jnp.mean(grad_hat, axis=-1, keepdims=True)
        - normed * jnp.mean(grad_hat * normed, axis=-1, keepdims=True)
    )


def exact_gelu(values):
    return jax.nn.gelu(values, approximate=False)


def split_heads(flat_rows):
    return flat_rows.reshape(-1, SEQ, flat_rows.shape[1] // HDIM, HDIM)


def project_first(first_all, w_query, b_query, w_key, w_value, b_value):
    queries = (jnp.dot(first_all, w_query, preferred_element_type=jnp.float32) + b_query).astype(
        jnp.bfloat16
    )
    keys_all = jnp.dot(first_all, w_key, preferred_element_type=jnp.float32).astype(jnp.bfloat16)
    values_all = (jnp.dot(first_all, w_value, preferred_element_type=jnp.float32) + b_value).astype(
        jnp.bfloat16
    )
    return (queries, keys_all, values_all)


def inner_layer(second_all, w_inner, b_inner):
    inner_pre = jnp.dot(second_all, w_inner, preferred_element_type=jnp.float32) + b_inner
    return (inner_pre, exact_gelu(inner_pre).astype(jnp.bfloat16))


def masked_scores(query_block, keys_all, valid_keys, score_scale):
    scores = (
        jnp.einsum("sqhe,skhe->shqk", query_block, keys_all, preferred_element_type=jnp.float32)
        * score_scale
    )
    return jnp.where(valid_keys[:, None, None, :], scores, NEG_LARGE)


def attention_forward(queries, keys_all, values_all, valid_keys, score_scale, block_rows):
    pieces = []
    log_sums = []
    for offset in range(0, SEQ, block_rows):
        scores = masked_scores(
            queries[:, offset : offset + block_rows], keys_all, valid_keys, score_scale
        )
        highest = jnp.max(scores, axis=-1, keepdims=True)
        weights = jnp.exp(scores - highest)
        totals = jnp.sum(weights, axis=-1, keepdims=True)
        softmax_low = (weights / totals).astype(jnp.bfloat16)
        mixture = jnp.einsum(
            "shqk,skhe->sqhe", softmax_low, values_all, preferred_element_type=jnp.float32
        )
        pieces.append(mixture.astype(jnp.bfloat16))
        log_sums.append((highest + jnp.log(totals))[..., 0])
    return (jnp.concatenate(pieces, axis=1), jnp.concatenate(log_sums, axis=2))


def attention_backward(
    queries, keys_all, values_all, grad_attended, log_sums, valid_keys, score_scale, block_rows
):
    grad_keys = jnp.zeros(keys_all.shape, jnp.float32)
    grad_values = jnp.zeros(values_all.shape, jnp.float32)
    grad_pieces = []
    for offset in range(0, SEQ, block_rows):
        query_block = queries[:, offset : offset + block_rows]
        grad_block = grad_attended[:, offset : offset + block_rows]
        scores = masked_scores(query_block, keys_all, valid_keys, score_scale)
        softmax_rows = jnp.exp(scores - log_sums[:, :, offset : offset + block_rows, None])
        grad_probs = jnp.einsum(
            "sqhe,skhe->shqk", grad_block, values_all, preferred_element_type=jnp.float32
        )
        centre = jnp.sum(softmax_rows * grad_probs, axis=-1, keepdims=True)
        grad_scores = (softmax_rows * (grad_probs - centre)).astype(jnp.bfloat16)
        grad_pieces.append(
            jnp.einsum("shqk,skhe->sqhe", grad_scores, keys_all, preferred_element_type=jnp.float32)
            * score_scale
        )
        grad_keys = (
            grad_keys
            + jnp.einsum(
                "shqk,sqhe->skhe", grad_scores, query_block, preferred_element_type=jnp.float32
            )
            * score_scale
        )
        grad_values = grad_values + jnp.einsum(
            "shqk,sqhe->skhe",
            softmax_rows.astype(jnp.bfloat16),
            grad_block,
            preferred_element_type=jnp.float32,
        )
    return (jnp.concatenate(grad_pieces, axis=1), grad_keys, grad_values)


def body(
    frames,
    cotangent,
    ada_gain,
    ada_shift,
    w_query,
    b_query,
    w_key,
    w_value,
    b_value,
    w_out,
    b_out,
    w_inner,
    b_inner,
    w_outer,
    b_outer,
    section_index,
    lengths,
    key_mask,
):
    rows_dev = frames.shape[0]
    model_width = frames.shape[1]
    seq_count = section_index.shape[0]
    score_scale = HDIM ** (-0.5)
    block_rows = min(512, SEQ)
    positions = lax.axis_index("tensor") * rows_dev + jnp.arange(rows_dev, dtype=jnp.int32)
    row_onehot = (
        positions[:, None] // SEQ == jnp.arange(seq_count, dtype=jnp.int32)[None, :]
    ).astype(jnp.float32)
    section_onehot = (
        section_index[:, None] - 2 == jnp.arange(ada_gain.shape[0], dtype=jnp.int32)[None, :]
    ).astype(jnp.float32)
    row_section = jnp.dot(row_onehot, section_onehot, precision=PRECISE)
    row_gain = jnp.dot(row_section, ada_gain, precision=PRECISE)
    row_shift = jnp.dot(row_section, ada_shift, precision=PRECISE)
    places = jnp.arange(SEQ, dtype=jnp.int32)
    valid_keys = (places[None, :] < lengths[:, None]) & (key_mask.reshape(seq_count, SEQ) > 0)
    inputs = frames.astype(jnp.float32)
    normed_one, inverse_one = normalize(inputs)
    first_low = (normed_one * row_gain[:, :model_width] + row_shift[:, :model_width]).astype(
        jnp.bfloat16
    )
    first_all = lax.all_gather(first_low, "tensor", axis=0, tiled=True)
    queries, keys_all, values_all = project_first(
        first_all, w_query, b_query, w_key, w_value, b_value
    )
    attended_heads, log_sums = attention_forward(
        split_heads(queries),
        split_heads(keys_all),
        split_heads(values_all),
        valid_keys,
        score_scale,
        block_rows,
    )
    attended = attended_heads.reshape(queries.shape)
    hidden = (
        inputs
        + lax.psum_scatter(
            jnp.dot(attended, w_out, preferred_element_type=jnp.float32),
            "tensor",
            scatter_dimension=0,
            tiled=True,
        )
        + b_out
    )
    normed_two, inverse_two = normalize(hidden)
    second_low = (normed_two * row_gain[:, model_width:] + row_shift[:, model_width:]).astype(
        jnp.bfloat16
    )
    second_all = lax.all_gather(second_low, "tensor", axis=0, tiled=True)
    inner_pre, activated = inner_layer(second_all, w_inner, b_inner)
    layer_out = (
        hidden
        + lax.psum_scatter(
            jnp.dot(activated, w_outer, preferred_element_type=jnp.float32).astype(jnp.bfloat16),
            "tensor",
            scatter_dimension=0,
            tiled=True,
        ).astype(jnp.float32)
        + b_outer
    ).astype(jnp.bfloat16)
    second_used, inner_used, activated_used = (second_all, inner_pre, activated)
    grad_all = lax.all_gather(cotangent, "tensor", axis=0, tiled=True)
    grad_w_outer = jnp.einsum(
        "gf,gd->fd", activated_used, grad_all, preferred_element_type=jnp.float32
    )
    grad_activated = jnp.einsum("gd,fd->gf", grad_all, w_outer, preferred_element_type=jnp.float32)
    unused_value, gelu_pull = jax.vjp(exact_gelu, inner_used)
    grad_inner = gelu_pull(grad_activated)[0].astype(jnp.bfloat16)
    grad_w_inner = jnp.einsum(
        "gd,gf->df", second_used, grad_inner, preferred_element_type=jnp.float32
    )
    grad_b_inner = jnp.sum(grad_inner.astype(jnp.float32), axis=0)
    grad_second = lax.psum_scatter(
        jnp.einsum("gf,df->gd", grad_inner, w_inner, preferred_element_type=jnp.float32),
        "tensor",
        scatter_dimension=0,
        tiled=True,
    )
    grad_out_rows = cotangent.astype(jnp.float32)
    grad_hidden = grad_out_rows + norm_back(
        grad_second * row_gain[:, model_width:], normed_two, inverse_two
    )
    grad_attn_low = grad_hidden.astype(jnp.bfloat16)
    grad_attn_all = lax.all_gather(grad_attn_low, "tensor", axis=0, tiled=True)
    first_used, queries_used, keys_used, values_used = (first_all, queries, keys_all, values_all)
    grad_w_out = jnp.einsum(
        "gc,gd->cd", attended, grad_attn_all, preferred_element_type=jnp.float32
    )
    grad_attended = jnp.einsum(
        "gd,cd->gc", grad_attn_all, w_out, preferred_element_type=jnp.float32
    ).astype(jnp.bfloat16)
    grad_q_heads, grad_k_heads, grad_v_heads = attention_backward(
        split_heads(queries_used),
        split_heads(keys_used),
        split_heads(values_used),
        split_heads(grad_attended),
        log_sums,
        valid_keys,
        score_scale,
        block_rows,
    )
    grad_queries = grad_q_heads.reshape(queries.shape).astype(jnp.bfloat16)
    grad_keys = grad_k_heads.reshape(queries.shape).astype(jnp.bfloat16)
    grad_values = grad_v_heads.reshape(queries.shape).astype(jnp.bfloat16)
    grad_w_query = jnp.einsum(
        "gd,gc->dc", first_used, grad_queries, preferred_element_type=jnp.float32
    )
    grad_w_key = jnp.einsum("gd,gc->dc", first_used, grad_keys, preferred_element_type=jnp.float32)
    grad_w_value = jnp.einsum(
        "gd,gc->dc", first_used, grad_values, preferred_element_type=jnp.float32
    )
    grad_b_query = jnp.sum(grad_queries.astype(jnp.float32), axis=0)
    grad_b_value = jnp.sum(grad_values.astype(jnp.float32), axis=0)
    total_rows = jnp.einsum("gc,dc->gd", grad_queries, w_query, preferred_element_type=jnp.float32)
    total_rows = total_rows + jnp.einsum(
        "gc,dc->gd", grad_keys, w_key, preferred_element_type=jnp.float32
    )
    grad_first = lax.psum_scatter(
        (
            total_rows
            + jnp.einsum("gc,dc->gd", grad_values, w_value, preferred_element_type=jnp.float32)
        ).astype(jnp.bfloat16),
        "tensor",
        scatter_dimension=0,
        tiled=True,
    ).astype(jnp.float32)
    frames_grad = grad_hidden + norm_back(
        grad_first * row_gain[:, :model_width], normed_one, inverse_one
    )
    gain_rows = jnp.concatenate([grad_first * normed_one, grad_second * normed_two], axis=1)
    shift_rows = jnp.concatenate([grad_first, grad_second], axis=1)
    gain_part = jnp.einsum("rs,rc->sc", row_section, gain_rows, precision=PRECISE)
    shift_part = jnp.einsum("rs,rc->sc", row_section, shift_rows, precision=PRECISE)
    grad_ada_gain, grad_ada_shift, grad_b_out, grad_b_outer = lax.psum(
        (gain_part, shift_part, jnp.sum(grad_hidden, axis=0), jnp.sum(grad_out_rows, axis=0)),
        ("dp", "tensor"),
    )
    (
        grad_w_query,
        grad_b_query,
        grad_w_key,
        grad_w_value,
        grad_b_value,
        grad_w_out,
        grad_w_inner,
        grad_b_inner,
        grad_w_outer,
    ) = lax.psum(
        (
            grad_w_query,
            grad_b_query,
            grad_w_key,
            grad_w_value,
            grad_b_value,
            grad_w_out,
            grad_w_inner,
            grad_b_inner,
            grad_w_outer,
        ),
        "dp",
    )
    return (
        layer_out,
        frames_grad,
        grad_ada_gain,
        grad_ada_shift,
        grad_w_query,
        grad_b_query,
        grad_w_key,
        grad_w_value,
        grad_b_value,
        grad_w_out,
        grad_b_out,
        grad_w_inner,
        grad_b_inner,
        grad_w_outer,
        grad_b_outer,
    )


def solution(mesh):
    return jax.shard_map(
        body,
        mesh=mesh,
        in_specs=(
            P(("dp", "tensor"), None),
            P(("dp", "tensor"), None),
            P(),
            P(),
            P(None, "tensor"),
            P("tensor"),
            P(None, "tensor"),
            P(None, "tensor"),
            P("tensor"),
            P("tensor", None),
            P(),
            P(None, "tensor"),
            P("tensor"),
            P("tensor", None),
            P(),
            P("dp"),
            P("dp"),
            P("dp"),
        ),
        out_specs=(
            P(("dp", "tensor"), None),
            P(("dp", "tensor"), None),
            P(),
            P(),
            P(None, "tensor"),
            P("tensor"),
            P(None, "tensor"),
            P(None, "tensor"),
            P("tensor"),
            P("tensor", None),
            P(),
            P(None, "tensor"),
            P("tensor"),
            P("tensor", None),
            P(),
        ),
        check_vma=False,
    )
```

profile of v0, /device:TPU:0, one launch (start us, length us, event | category | flops | bytes accessed | tf_op | source)
XLA Modules:
  0.0 919.6 jit_solution(3665876718089598544)
XLA Ops:
  10.8 2.7 fusion.64
  13.5 2.8 fusion.62
  19.9 24.3 %all-gather.5.cloned.1.call-done = bf16[1024,1024]{1,0:T(8,128)(2,1)} async-done(((bf16[256,1024]{1,0:T(8,128)(2,1)}), bf16[1024,1024]{1,0:T(8,128)(2,1)}) %all-gather.5.cloned.1.call-update) | async-done | bytes 2097168 | tf_op jit(solution)/shard_map/all_gather | solution.py:158
  44.2 2.3 convolution_convert_fusion.2
  46.6 2.6 fusion.37
  50.5 2.3 fusion.18
  52.9 3.8 fusion
  57.5 2.5 fusion.48
  60.0 2.5 fusion.49
  63.4 2.8 fusion.96
  66.3 44.7 %reduce-scatter.5.cloned.1.call-done = f32[256,1024]{1,0:T(8,128)} async-done(((f32[1024,1024]{1,0:T(8,128)}), f32[256,1024]{1,0:T(8,128)}) %reduce-scatter.5.cloned.1.call-update) | async-done | bytes 1048592 | tf_op jit(solution)/shard_map/reduce_scatter | solution.py:173
  113.0 2.3 fusion.58
  116.2 21.9 %all-gather.7.cloned.1.call-done = bf16[1024,1024]{1,0:T(8,128)(2,1)} async-done(((bf16[256,1024]{1,0:T(8,128)(2,1)}), bf16[1024,1024]{1,0:T(8,128)(2,1)}) %all-gather.7.cloned.1.call-update) | async-done | bytes 2097168 | tf_op jit(solution)/shard_map/all_gather | solution.py:185
  138.1 6.6 fusion.97
  144.6 17.4 %all-gather.9.cloned.1.call-done = bf16[1024,1024]{1,0:T(8,128)(2,1)} async-done(((bf16[256,1024]{1,0:T(8,128)(2,1)}), bf16[1024,1024]{1,0:T(8,128)(2,1)}) %all-gather.9.cloned.1.call-update) | async-done | bytes 2097168 | tf_op jit(solution)/shard_map/all_gather | solution.py:198
  162.1 14.8 %convert_reduce_fusion = (f32[1024]{0:T(1024)S(1)}, bf16[1024,1024]{1,0:T(8,128)(2,1)S(1)}, f32[1024,1024]{1,0:T(8,128)}) fusion(f32[1024,1024]{1,0:T(8,128)} %fusion.97, f32[1024]{0:T(1024)S(1)} %copy-done.50, bf16[1024,1024]{1,0:T(8,128)(2,1)} %all-gather.9.cloned.1.call-done, bf16[1024,1024]{1,0:T(8,128)(2,1)S(1)} %copy-done), kind=kOutput, calls=%fused_computation.20 | convolution fusion | flops 2226125824 | bytes 14688256 | tf_op jit(solution)/shard_map/gd,fd->gf/dot_general | solution.py:202
  178.2 4.4 fusion.98
  182.6 4.6 multiply_convert_fusion.2
  188.6 3.7 convolution_convert_fusion
  192.3 35.0 %reduce-scatter.9.cloned.1.call-done = f32[256,1024]{1,0:T(8,128)} async-done(((f32[1024,1024]{1,0:T(8,128)}), f32[256,1024]{1,0:T(8,128)}) %reduce-scatter.9.cloned.1.call-update) | async-done | bytes 1048592 | tf_op jit(solution)/shard_map/reduce_scatter | solution.py:209
  227.3 1.9 fusion.91
  229.2 32.3 %reduce-scatter.7.cloned.1.call-done = bf16[256,1024]{1,0:T(8,128)(2,1)} async-done(((bf16[1024,1024]{1,0:T(8,128)(2,1)}), bf16[256,1024]{1,0:T(8,128)(2,1)}) %reduce-scatter.7.cloned.1.call-update) | async-done | bytes 524304 | tf_op jit(solution)/shard_map/reduce_scatter | solution.py:189
  261.5 3.8 fusion.93
  267.5 22.4 %all-gather.11.cloned.1.call-done = bf16[1024,1024]{1,0:T(8,128)(2,1)} async-done(((bf16[256,1024]{1,0:T(8,128)(2,1)}), bf16[1024,1024]{1,0:T(8,128)(2,1)}) %all-gather.11.cloned.1.call-update) | async-done | bytes 2097168 | tf_op jit(solution)/shard_map/all_gather | solution.py:220
  289.9 2.6 convolution_convert_fusion.1
  292.5 5.4 fusion.71
  297.9 2.9 fusion.5
  300.8 9.0 multiply_reduce_fusion.1
  309.8 8.4 multiply_convert_fusion.1
  320.8 2.2 convert_reduce_fusion.3
  327.4 2.1 add_convert_fusion
  329.9 6.8 fusion.106
  336.7 4.4 fusion.105
  342.9 1.7 fusion.103
  344.6 1.7 fusion.101
  346.3 14.5 %reduce-scatter.11.cloned.1.call-done = bf16[256,1024]{1,0:T(8,128)(2,1)} async-done(((bf16[1024,1024]{1,0:T(8,128)(2,1)}), bf16[256,1024]{1,0:T(8,128)(2,1)}) %reduce-scatter.11.cloned.1.call-update) | async-done | bytes 524304 | tf_op jit(solution)/shard_map/reduce_scatter | solution.py:254
  360.9 2.0 fusion.66
  363.0 3.0 fusion.20
  366.1 1.8 fusion.24
  367.9 1.7 fusion.102
  369.9 22.4 %all-reduce.1 = (f32[256]{0:T(256)}, f32[256]{0:T(256)}, f32[1024]{0:T(1024)}) all-reduce(f32[256]{0:T(256)S(1)} %reduce_sum.170, f32[256]{0:T(256)S(1)} %reduce_sum.172, f32[1024]{0:T(1024)S(1)} %get-tuple-element.38), channel_id=1, replica_groups=mesh['dp'=8,'tensor'=4] {'dp'}, use_global_device_ids=true, to_apply=%region_22.23 | all-reduce | flops 1536 | bytes 12288 | tf_op jit(solution)/shard_map/psum | solution.py:284
  392.3 2.6 fusion.55
  394.9 96.2 %all-reduce.6.cloned.1.call-done = (f32[7,2048]{1,0:T(8,128)}, f32[7,2048]{1,0:T(8,128)}, f32[1024]{0:T(1024)}, f32[1024]{0:T(1024)}) async-done(((f32[7,2048]{1,0:T(8,128)}, f32[7,2048]{1,0:T(8,128)}, f32[1024]{0:T(1024)}, f32[1024]{0:T(1024)}), (f32[7,2048]{1,0:T(8,128)}, f32[7,2048]{1,0:T(8,128)}, f32[1024]{0:T(1024)}, f32[1024]{0:T(1024)})) %all-reduce.6.cloned.1.call-update) | async-done | bytes 122896 | tf_op jit(solution)/shard_map/psum | solution.py:270
  491.1 404.6 %all-reduce.8.cloned.1.call-done = (f32[1024,256]{1,0:T(8,128)}, f32[1024,256]{1,0:T(8,128)}, f32[1024,256]{1,0:T(8,128)}, f32[256,1024]{1,0:T(8,128)}, f32[1024,1024]{1,0:T(8,128)}, /*index=5*/f32[1024,1024]{1,0:T(8,128)}) async-done(((f32[1024,256]{1,0:T(8,128)}, f32[1024,256]{1,0:T(8,128)}, f32[1024,256]{1,0:T(8,128)}, f32[256,1024]{1,0:T(8,128)}, f32[1024,1024]{1,0:T(8,128)}, ...) | async-done | bytes 12582928 | tf_op jit(solution)/shard_map/psum | solution.py:284
  898.8 2.4 copy.47
  901.2 2.3 copy.48
  906.0 2.1 copy.52
  909.7 2.0 copy.53
  (191 shorter events, 33.5 us)
Async XLA Ops:
  7.2 154.9 %copy-start = (bf16[1024,1024]{1,0:T(8,128)(2,1)S(1)}, bf16[1024,1024]{1,0:T(8,128)(2,1)}, u32[]{:S(2)}) copy-start(bf16[1024,1024]{1,0:T(8,128)(2,1)} %param.31) | copy-start | bytes 6291460
  7.2 10.4 %copy-start.10 = (bf16[256,1024]{1,0:T(8,128)(2,1)S(1)}, bf16[256,1024]{1,0:T(8,128)(2,1)}, u32[]{:S(2)}) copy-start(bf16[256,1024]{1,0:T(8,128)(2,1)} %param.18) | copy-start | bytes 1572868
  7.2 37.0 %all-gather.5.cloned.1.call-start = ((), (), s32[]{:S(2)}) async-start(), calls=%async_computation.4 | async-start | bytes 2621440 | tf_op jit(solution)/shard_map/all_gather | solution.py:158
  8.1 10.6 %copy-start.47 = (f32[7]{0:T(128)}, f32[7]{0:T(128)S(1)}, u32[]{:S(2)}) copy-start(f32[7]{0:T(128)S(1)} %compare_convert_fusion) | copy-start | bytes 88
  8.1 5.3 copy-start.43
  9.3 6.9 copy-start.41
  9.4 10.6 %copy-start.51 = (s32[1024]{0:T(1024)S(1)}, s32[1024]{0:T(1024)}, u32[]{:S(2)}) copy-start(s32[1024]{0:T(1024)} %param.35) | copy-start | bytes 12292
  9.4 34.8 %copy-start.36 = (bf16[1024,256]{1,0:T(8,128)(2,1)S(1)}, bf16[1024,256]{1,0:T(8,128)(2,1)}, u32[]{:S(2)}) copy-start(bf16[1024,256]{1,0:T(8,128)(2,1)} %param.24) | copy-start | bytes 1572868
  10.8 5.5 copy-start.45
  13.5 33.1 %copy-start.57 = (f32[256]{0:T(256)S(1)}, f32[256]{0:T(256)}, u32[]{:S(2)}) copy-start(f32[256]{0:T(256)} %param.23) | copy-start | bytes 3076
  18.8 92.2 %reduce-scatter.5.cloned.1.call-start = ((), (), s32[]{:S(2)}) async-start(), calls=%async_computation.5 | async-start | bytes 5242880 | tf_op jit(solution)/shard_map/reduce_scatter | solution.py:173
  50.5 9.5 %copy-start.2 = (f32[4,512,1024]{2,1,0:T(8,128)}, f32[4,512,1024]{2,1,0:T(8,128)S(1)}, u32[]{:S(2)}) copy-start(f32[4,512,1024]{2,1,0:T(8,128)S(1)} %fusion.69) | copy-start | bytes 25165828
  66.2 44.8 %copy-start.49 = (f32[1024]{0:T(1024)S(1)}, f32[1024]{0:T(1024)}, u32[]{:S(2)}) copy-start(f32[1024]{0:T(1024)} %param.28) | copy-start | bytes 12292
  66.2 71.9 %all-gather.7.cloned.1.call-start = ((), (), s32[]{:S(2)}) async-start(), calls=%async_computation.6 | async-start | bytes 2621440 | tf_op jit(solution)/shard_map/all_gather | solution.py:185
  115.4 46.7 %all-gather.9.cloned.1.call-start = ((), (), s32[]{:S(2)}) async-start(), calls=%async_computation.8 | async-start | bytes 2621440 | tf_op jit(solution)/shard_map/all_gather | solution.py:198
  115.9 46.2 %copy-start.50 = (f32[1024]{0:T(1024)S(1)}, f32[1024]{0:T(1024)}, u32[]{:S(2)}) copy-start(f32[1024]{0:T(1024)} %param.30) | copy-start | bytes 12292
  115.9 111.4 %reduce-scatter.9.cloned.1.call-start = ((), (), s32[]{:S(2)}) async-start(), calls=%async_computation.9 | async-start | bytes 5242880 | tf_op jit(solution)/shard_map/reduce_scatter | solution.py:209
  162.1 16.1 %copy-start.55 = (bf16[1024,1024]{1,0:T(8,128)(2,1)S(1)}, bf16[1024,1024]{1,0:T(8,128)(2,1)}, u32[]{:S(2)}) copy-start(bf16[1024,1024]{1,0:T(8,128)(2,1)} %param.29) | copy-start | bytes 6291460
  182.6 78.9 %reduce-scatter.7.cloned.1.call-start = ((), (), s32[]{:S(2)}) async-start(), calls=%async_computation.7 | async-start | bytes 2621440 | tf_op jit(solution)/shard_map/reduce_scatter | solution.py:189
  192.2 69.3 %copy-start.8 = (f32[256,2048]{1,0:T(8,128)S(1)}, f32[256,2048]{1,0:T(8,128)}, u32[]{:S(2)}) copy-start(f32[256,2048]{1,0:T(8,128)} %copy-done.6) | copy-start | bytes 6291460
  192.2 69.3 %copy-start.54 = (f32[1024]{0:T(1024)S(1)}, f32[1024]{0:T(1024)}, u32[]{:S(2)}) copy-start(f32[1024]{0:T(1024)} %param.32) | copy-start | bytes 12292
  192.2 97.7 %all-gather.11.cloned.1.call-start = ((), (), s32[]{:S(2)}) async-start(), calls=%async_computation.10 | async-start | bytes 2621440 | tf_op jit(solution)/shard_map/all_gather | solution.py:220
  265.3 27.2 %copy-start.28 = (bf16[1024,256]{0,1:T(8,128)(2,1)S(1)}, bf16[1024,256]{0,1:T(8,128)(2,1)}, u32[]{:S(2)}) copy-start(bf16[1024,256]{0,1:T(8,128)(2,1)} %copy-done.27) | copy-start | bytes 1572868
  267.2 93.7 %reduce-scatter.11.cloned.1.call-start = ((), (), s32[]{:S(2)}) async-start(), calls=%async_computation.11 | async-start | bytes 2621440 | tf_op jit(solution)/shard_map/reduce_scatter | solution.py:254
  289.9 8.0 slice-start
  292.5 5.4 slice-start.1
  292.5 8.3 slice-start.2
  309.8 8.4 copy-start.15
  329.6 161.5 %all-reduce.6.cloned.1.call-start = ((), (), s32[]{:S(2)}) async-start(), calls=%async_computation.12 | async-start | bytes 278528 | tf_op jit(solution)/shard_map/psum | solution.py:270
  329.9 6.8 copy-start.56
  329.9 6.8 copy-start.61
  336.7 6.2 copy-start.5
  336.7 6.2 copy-start.31
  342.8 18.1 %copy-start.11 = (bf16[256,1024]{1,0:T(8,128)(2,1)S(1)}, bf16[256,1024]{1,0:T(8,128)(2,1)}, u32[]{:S(2)}) copy-start(bf16[256,1024]{1,0:T(8,128)(2,1)} %param.18) | copy-start | bytes 1572868
  342.8 18.1 %copy-start.42 = (f32[256]{0:T(256)S(1)}, f32[256]{0:T(256)}, u32[]{:S(2)}) copy-start(f32[256]{0:T(256)} %copy-done.41) | copy-start | bytes 3076
  342.8 18.1 %copy-start.46 = (f32[256]{0:T(256)S(1)}, f32[256]{0:T(256)}, u32[]{:S(2)}) copy-start(f32[256]{0:T(256)} %copy-done.45) | copy-start | bytes 3076
  344.6 18.3 %copy-start.44 = (f32[256]{0:T(256)S(1)}, f32[256]{0:T(256)}, u32[]{:S(2)}) copy-start(f32[256]{0:T(256)} %copy-done.43) | copy-start | bytes 3076
  344.6 18.3 %copy-start.48 = (f32[7]{0:T(128)S(1)}, f32[7]{0:T(128)}, u32[]{:S(2)}) copy-start(f32[7]{0:T(128)} %copy-done.47) | copy-start | bytes 88
  360.9 5.1 copy-start.21
  360.9 5.2 copy-start.13
  367.9 527.8 %all-reduce.8.cloned.1.call-start = ((), (), s32[]{:S(2)}) async-start(), calls=%async_computation.13 | async-start | bytes 25165824 | tf_op jit(solution)/shard_map/psum | solution.py:284
  369.7 22.6 %copy-start.9 = (f32[256,2048]{1,0:T(8,128)S(1)}, f32[256,2048]{1,0:T(8,128)}, u32[]{:S(2)}) copy-start(f32[256,2048]{1,0:T(8,128)} %copy-done.6) | copy-start | bytes 6291460
  369.7 22.6 %copy-start.22 = (bf16[256,1024]{1,0:T(8,128)(2,1)S(1)}, bf16[256,1024]{1,0:T(8,128)(2,1)}, u32[]{:S(2)}) copy-start(bf16[256,1024]{1,0:T(8,128)(2,1)} %reduce-scatter.11.cloned.1.call-done) | copy-start | bytes 1572868
  895.7 7.8 copy-start.34
  895.7 8.8 copy-start.33
  898.8 6.6 copy-start.53
  898.8 7.2 copy-start.24
  906.0 6.3 copy-start.1
  (28 other events, 72.2 us)
Sparse Core Ops, SparseCore 0:
  18.9 25.2 all-gather.4
  66.3 44.5 reduce-scatter.4
  115.5 22.5 all-gather.6
  139.5 22.5 all-gather.8
  182.7 44.5 reduce-scatter.8
  230.3 31.1 reduce-scatter.6
  267.3 22.5 all-gather.10
  329.7 31.1 reduce-scatter.10
  368.1 122.9 all-reduce.5
  497.5 398.1 all-reduce.7
where the time goes:
time: 923 us; the launch traced here: 920 us
  waiting for transfers between devices  714 us (77%)
  matrix products  105 us (11%)
  other arithmetic  36.3 us (4%)
  local copies, waits for them, and re-layouts  23.4 us (3%)
  blocking collectives  22.4 us (2%)
  between operations  16.8 us (2%)
    psum x1, waiting for transfers between devices, body(): lax.psum((grad_w_query, grad_b_query, grad_w_key, grad_w_value, grad_b_va...  405 us
    psum x1, waiting for transfers between devices, body(): lax.psum((gain_part, shift_part, jnp.sum(grad_hidden, axis=0), jnp.sum(gr...  96.2 us
    reduce_scatter x1, waiting for transfers between devices, body(): lax.psum_scatter(jnp.dot(attended, w_out, preferred_element_type=jnp.floa...  44.7 us
    reduce_scatter x1, waiting for transfers between devices, body(): lax.psum_scatter(jnp.einsum('gf,df->gd', grad_inner, w_inner, preferred_e...  35 us
    reduce_scatter x1, waiting for transfers between devices, body(): lax.psum_scatter(jnp.dot(activated, w_outer, preferred_element_type=jnp.f...  32.3 us
    all_gather x1, waiting for transfers between devices, body(): first_all = lax.all_gather(first_low, 'tensor', axis=0, tiled=True)  24.3 us
    unnamed x142, local copies, waits for them, and re-layouts  23.3 us
    all_gather x1, waiting for transfers between devices, body(): grad_attn_all = lax.all_gather(grad_attn_low, 'tensor', axis=0, tiled=True)  22.4 us
  transfers between devices with their start and end apart: 10, of which 10 were waited for; matrix products, arithmetic and copies ran while one was open for 4% of the time, Pallas kernels for 0%

commit v1 on v0

v1 whole, which is shorter than its diff:
```python
import functools

import jax
import jax.numpy as jnp
from jax import lax
from jax.experimental import pallas as pl
from jax.experimental.pallas import tpu as pltpu
from jax.sharding import PartitionSpec as P

HDIM = 64
SEQ = 1024
EPSILON = 1e-05
NEG_LARGE = -1e30
F32 = jnp.float32
BF16 = jnp.bfloat16
MESH = pl.DeviceIdType.MESH
VMEM_LIMIT = 60 * 1024 * 1024


def places():
    dp = lax.axis_index("dp")
    me = lax.axis_index("tensor")
    sib = me + 1 - 2 * (me % 2)
    across = (me + 2) % 4
    diag = (sib + 2) % 4
    return dp, me, sib, across, diag


def greet(partners):
    barrier = pltpu.get_barrier_semaphore()
    for partner in partners:
        pl.semaphore_signal(barrier, inc=1, device_id=partner, device_id_type=MESH)
    pl.semaphore_wait(barrier, len(partners))


def remote(src, dst, send, recv, device):
    return pltpu.make_async_remote_copy(
        src_ref=src, dst_ref=dst, send_sem=send, recv_sem=recv, device_id=device, device_id_type=MESH
    )


def whole_vmem(count):
    return [pl.BlockSpec(memory_space=pltpu.VMEM)] * count


PARTS = 4


def gather_kernel(x_ref, o_ref, send, recv):
    dp, me, sib, across, diag = places()
    rows = x_ref.shape[0]
    part = rows // PARTS
    greet([(dp, sib), (dp, across)])
    copies = []
    for i in range(PARTS):
        at = pl.multiple_of(me * rows + i * part, part)
        copies.append(
            remote(x_ref.at[pl.ds(i * part, part)], o_ref.at[pl.ds(at, part)], send.at[i], recv.at[i], (dp, across))
        )
        copies[-1].start()
    mine = pl.ds(pl.multiple_of(me * rows, rows), rows)
    copies.append(remote(x_ref, o_ref.at[mine], send.at[PARTS], recv.at[PARTS], (dp, sib)))
    copies[-1].start()
    o_ref[mine, :] = x_ref[...]
    for i in range(PARTS):
        copies[i].wait_recv()
        there = pl.ds(pl.multiple_of(across * rows + i * part, part), part)
        j = PARTS + 1 + i
        copies.append(remote(o_ref.at[there], o_ref.at[there], send.at[j], recv.at[j], (dp, sib)))
        copies[-1].start()
    for i, copy in enumerate(copies):
        if i >= PARTS:
            copy.wait_recv()
        copy.wait_send()


def tensor_gather(block, cid):
    rows, width = block.shape
    return pl.pallas_call(
        gather_kernel,
        out_shape=jax.ShapeDtypeStruct((rows * 4, width), block.dtype),
        in_specs=whole_vmem(1),
        out_specs=pl.BlockSpec(memory_space=pltpu.VMEM),
        scratch_shapes=[pltpu.SemaphoreType.DMA((2 * PARTS + 1,))] * 2,
        compiler_params=pltpu.CompilerParams(collective_id=cid, has_side_effects=True, vmem_limit_bytes=VMEM_LIMIT),
        name="tensor_gather_%d" % cid,
    )(block)


def scatter_kernel(p_ref, o_ref, from_sib, chip_sum, landed, send, recv):
    dp, me, sib, across, diag = places()
    rows = p_ref.shape[0] // 4
    part = rows // PARTS
    greet([(dp, sib), (dp, across)])

    def at(owner, i):
        return pl.ds(pl.multiple_of(owner * rows + i * part, part), part)

    first, last = [], []
    for i in range(PARTS):
        here = pl.ds(i * part, part)
        first.append(remote(p_ref.at[at(diag, i)], from_sib.at[0, here], send.at[i], recv.at[i], (dp, sib)))
        first[-1].start()
    for i in range(PARTS):
        here = pl.ds(i * part, part)
        j = PARTS + i
        last.append(remote(p_ref.at[at(sib, i)], from_sib.at[1, here], send.at[j], recv.at[j], (dp, sib)))
        last[-1].start()
    crossing = []
    for i in range(PARTS):
        here = pl.ds(i * part, part)
        j = 2 * PARTS + i
        first[i].wait_recv()
        chip_sum[here, :] = (p_ref[at(across, i), :].astype(F32) + from_sib[0, here, :].astype(F32)).astype(BF16)
        crossing.append(remote(chip_sum.at[here], landed.at[here], send.at[j], recv.at[j], (dp, across)))
        crossing[-1].start()
    for i in range(PARTS):
        here = pl.ds(i * part, part)
        last[i].wait_recv()
        o_ref[here, :] = p_ref[at(me, i), :].astype(F32) + from_sib[1, here, :].astype(F32)
    for i in range(PARTS):
        here = pl.ds(i * part, part)
        crossing[i].wait_recv()
        o_ref[here, :] = o_ref[here, :] + landed[here, :].astype(F32)
    for copy in first + last + crossing:
        copy.wait_send()


def tensor_scatter(partial, cid):
    rows, width = partial.shape[0] // 4, partial.shape[1]
    return pl.pallas_call(
        scatter_kernel,
        out_shape=jax.ShapeDtypeStruct((rows, width), F32),
        in_specs=whole_vmem(1),
        out_specs=pl.BlockSpec(memory_space=pltpu.VMEM),
        scratch_shapes=[
            pltpu.VMEM((2, rows, width), BF16),
            pltpu.VMEM((rows, width), BF16),
            pltpu.VMEM((rows, width), BF16),
            pltpu.SemaphoreType.DMA((3 * PARTS,)),
            pltpu.SemaphoreType.DMA((3 * PARTS,)),
        ],
        compiler_params=pltpu.CompilerParams(collective_id=cid, has_side_effects=True, vmem_limit_bytes=VMEM_LIMIT),
        name="tensor_scatter_%d" % cid,
    )(partial)


def dp_lines(count):
    sizes, limit = [], 2
    while count > 1:
        size = min(count, limit)
        sizes.append(size)
        count //= size
        limit *= 2
    return sizes


class Line:
    def __init__(self, size, stride, dp, me):
        self.size = size
        self.place = (dp // stride) % size
        self.right = (jnp.minimum(dp + stride, dp + (size - 1 - self.place) * stride), me)
        self.left = (jnp.maximum(dp - stride, dp - self.place * stride), me)
        self.pair = (dp + stride - 2 * stride * (dp // stride % 2), me)


def lines_of(count, dp, me):
    found, stride = [], 1
    for size in dp_lines(count):
        found.append(Line(size, stride, dp, me))
        stride *= size
    return found


def chunk_sems(count):
    sizes = dp_lines(count)
    return 1 + sizes[1] + sum(4 * size for size in sizes[1:])


def chunk_scratch(count, rows, width):
    sizes = dp_lines(count)
    shapes = [pltpu.VMEM((rows // 2, width), BF16), pltpu.VMEM((rows // 2, width), BF16)]
    part = rows // 2
    for size in sizes[1:]:
        part //= size
        shapes += [pltpu.VMEM((size, part, width), BF16)] * 2
    return shapes


def sum_chunk(lines, x_ref, o_ref, columns, scratch, send, recv):
    rows = x_ref.shape[0]
    got, own = scratch[0], scratch[1]
    buffers = [scratch[2 + 2 * i : 4 + 2 * i] for i in range(len(lines) - 1)]
    pair = lines[0]
    half = rows // 2
    started = []
    used = [0]

    def slots(count):
        used[0] += count
        return used[0] - count

    def go(copy, condition=None):
        if condition is None:
            copy.start()
        else:
            pl.when(condition)(lambda: copy.start())
        started.append((copy, condition))

    def when(condition, body):
        pl.when(condition)(body)

    mine = pl.multiple_of(pair.place * half, half)
    other = pl.multiple_of(half - pair.place * half, half)
    slot = slots(1)
    first = remote(x_ref.at[pl.ds(other, half), columns], got, send.at[slot], recv.at[slot], pair.pair)
    go(first)
    yield
    first.wait_recv()
    own[...] = (x_ref[pl.ds(mine, half), columns].astype(F32) + got[...].astype(F32)).astype(BF16)
    base = 0
    size_now = half
    for line, (to_right, to_left) in zip(lines[1:], buffers):
        n, z = line.size, line.place
        part = size_now // n
        right_slot, left_slot = slots(n), slots(n)
        bases = base

        def piece(o, part=part, bases=bases):
            return pl.ds(pl.multiple_of(bases + o * part, part), part)

        for j in range(n - 1, 0, -1):
            for way in (0, 1):
                o = z + j if way == 0 else z - j
                inside = (o < n) if way == 0 else (o >= 0)
                buffer = to_right if way == 0 else to_left
                at_end = (z == 0) if way == 0 else (z == n - 1)
                slot = (right_slot if way == 0 else left_slot) + jnp.clip(o, 0, n - 1)
                o = jnp.clip(o, 0, n - 1)
                there = line.right if way == 0 else line.left
                copy = remote(own.at[piece(o)], buffer.at[o], send.at[slot], recv.at[slot], there)
                onward = remote(buffer.at[o], buffer.at[o], send.at[slot], recv.at[slot], there)
                go(copy, inside & at_end)

                def pass_on(buffer=buffer, o=o, onward=onward, piece=piece):
                    onward.wait_recv()
                    buffer[o] = (buffer[o].astype(F32) + own[piece(o), :].astype(F32)).astype(BF16)
                    onward.start()

                when(inside & jnp.logical_not(at_end), pass_on)
                started.append((onward, inside & jnp.logical_not(at_end)))
            yield

        def take(buffer, slot, line=line, piece=piece, z=z):
            remote(buffer.at[z], buffer.at[z], send.at[slot + z], recv.at[slot + z], line.right).wait_recv()
            own[piece(z), :] = (own[piece(z), :].astype(F32) + buffer[z].astype(F32)).astype(BF16)

        when(z > 0, functools.partial(take, to_right, right_slot))
        when(z < n - 1, functools.partial(take, to_left, left_slot))
        base = bases + z * part
        size_now = part
    final = pl.ds(pl.multiple_of(mine + base, size_now), size_now)
    o_ref[final, columns] = own[pl.ds(pl.multiple_of(base, size_now), size_now), :]
    region = mine + base
    for level in range(len(lines) - 1, 0, -1):
        line = lines[level]
        n, z = line.size, line.place
        part = size_now
        base_region = region - z * part
        right_slot, left_slot = slots(n), slots(n)
        pair_slot = slots(n) if level == 1 else None

        def piece(o, part=part, base_region=base_region):
            return pl.ds(pl.multiple_of(base_region + o * part, part), part)

        def copy_of(o, slot, there, piece=piece):
            ref = o_ref.at[piece(o), columns]
            return remote(ref, ref, send.at[slot + o], recv.at[slot + o], there)

        go(copy_of(z, right_slot, line.right), z < n - 1)
        go(copy_of(z, left_slot, line.left), z > 0)
        if level == 1:
            go(copy_of(z, pair_slot, pair.pair))
        yield
        for j in range(1, n):
            for way in (0, 1):
                o = z - j if way == 0 else z + j
                inside = (o >= 0) if way == 0 else (o < n)
                goes_on = (z < n - 1) if way == 0 else (z > 0)
                o = jnp.clip(o, 0, n - 1)
                slot = right_slot if way == 0 else left_slot
                there = line.right if way == 0 else line.left
                copy = copy_of(o, slot, there)
                when(inside, lambda copy=copy: copy.wait_recv())
                go(copy, inside & goes_on)
                if level == 1:
                    go(copy_of(o, pair_slot, pair.pair), inside)
            yield
        region = base_region
        size_now = part * n
        if level == 1:
            for o in range(n):
                ref = o_ref.at[pl.ds(pl.multiple_of(other + o * part, part), part), columns]
                remote(ref, ref, send.at[pair_slot + o], recv.at[pair_slot + o], pair.pair).wait_recv()
    for copy, condition in started:
        if condition is None:
            copy.wait_send()
        else:
            when(condition, lambda copy=copy: copy.wait_send())


def run_skewed(makers):
    makers = list(makers)
    running = []
    while makers or running:
        if makers:
            running.append(makers.pop(0)())
        still = []
        for generator in running:
            try:
                next(generator)
                still.append(generator)
            except StopIteration:
                pass
        running = still


def dp_sum_kernel(count, widths, *refs):
    arrays = len(widths)
    ins, rest = refs[:arrays], refs[arrays:]
    vec_ref, bias_ref, pick_ref = rest[:3]
    outs, rest = rest[3 : 3 + arrays], rest[3 + arrays :]
    small_out, rest = rest[0], rest[1:]
    small_in, vec_got, vec_send, vec_recv = rest[:4]
    rest = rest[4:]
    dp, me, sib, across, diag = places()
    lines = lines_of(count, dp, me)
    others = [lines[0].pair]
    near = [(dp, sib), (dp, across), (dp, diag)]
    barrier = pltpu.get_barrier_semaphore()
    for partner in near + others:
        pl.semaphore_signal(barrier, inc=1, device_id=partner, device_id_type=MESH)
    waits = len(near) + len(others)
    for line in lines[1:]:
        has_right = line.place < line.size - 1
        has_left = line.place > 0
        for partner, has in ((line.right, has_right), (line.left, has_left)):
            pl.when(has)(
                lambda partner=partner: pl.semaphore_signal(
                    barrier, inc=1, device_id=partner, device_id_type=MESH
                )
            )
        waits = waits + has_right.astype(jnp.int32) + has_left.astype(jnp.int32)
    pl.semaphore_wait(barrier, waits)
    vec_copies = []
    for i, device in enumerate(near):
        vec_copies.append(remote(vec_ref, vec_got.at[i], vec_send.at[i], vec_recv.at[i], device))
        vec_copies[-1].start()

    per = 2 + 2 * (len(lines) - 1)
    makers = []
    for array in range(arrays):
        wide = ins[array].shape[1]
        for start in range(0, wide, widths[array]):
            scratch, rest = rest[:per], rest[per:]
            send, recv = rest[:2]
            rest = rest[2:]
            makers.append(
                functools.partial(
                    sum_chunk, lines, ins[array], outs[array], pl.ds(start, widths[array]), scratch, send, recv
                )
            )

    def small():
        for copy in vec_copies:
            copy.wait_recv()
        total = vec_ref[...] + vec_got[0] + vec_got[1] + vec_got[2]
        sections = pick_ref.shape[0]
        for s in range(sections):
            small_in[pl.ds(32 * s, 32), :] = (total[0:32] * pick_ref[s : s + 1, :]).astype(BF16)
        small_in[pl.ds(32 * sections, 16), :] = total[32:48].astype(BF16)
        small_in[pl.ds(32 * sections + 16, 16), :] = bias_ref[...].astype(BF16)
        done = 32 * sections + 32
        if done < small_in.shape[0]:
            small_in[pl.ds(done, small_in.shape[0] - done), :] = jnp.zeros((small_in.shape[0] - done, 128), BF16)
        yield from sum_chunk(lines, small_in, small_out, slice(None), rest[:per], rest[per], rest[per + 1])

    run_skewed(makers + [small])
    for copy in vec_copies:
        copy.wait_send()


def dp_sum(count, grads, widths, vec, bias, pick, cid):
    small_rows = max(16 * count, -(-(32 * pick.shape[0] + 32) // (16 * count)) * 16 * count)
    sems = chunk_sems(count)
    scratch = [
        pltpu.VMEM((small_rows, 128), BF16),
        pltpu.VMEM((3,) + vec.shape, F32),
        pltpu.SemaphoreType.DMA((3,)),
        pltpu.SemaphoreType.DMA((3,)),
    ]
    for grad, width in zip(grads, widths):
        for _ in range(0, grad.shape[1], width):
            scratch += chunk_scratch(count, grad.shape[0], width)
            scratch += [pltpu.SemaphoreType.DMA((sems,))] * 2
    scratch += chunk_scratch(count, small_rows, 128)
    scratch += [pltpu.SemaphoreType.DMA((sems,))] * 2
    return pl.pallas_call(
        functools.partial(dp_sum_kernel, count, tuple(widths)),
        out_shape=[jax.ShapeDtypeStruct(g.shape, BF16) for g in grads]
        + [jax.ShapeDtypeStruct((small_rows, 128), BF16)],
        in_specs=whole_vmem(len(grads) + 3),
        out_specs=whole_vmem(len(grads) + 1),
        scratch_shapes=scratch,
        compiler_params=pltpu.CompilerParams(collective_id=cid, has_side_effects=True, vmem_limit_bytes=VMEM_LIMIT),
        name="dp_sum",
    )(*grads, vec, bias, pick)


def normalize(row_block):
    centered = row_block - jnp.mean(row_block, axis=-1, keepdims=True)
    inverse = lax.rsqrt(jnp.mean(centered * centered, axis=-1, keepdims=True) + EPSILON)
    return (centered * inverse, inverse)


def norm_back(grad_hat, normed, inverse):
    return inverse * (
        grad_hat
        - jnp.mean(grad_hat, axis=-1, keepdims=True)
        - normed * jnp.mean(grad_hat * normed, axis=-1, keepdims=True)
    )


def exact_gelu(values):
    return jax.nn.gelu(values, approximate=False)


def split_heads(flat_rows):
    return flat_rows.reshape(-1, SEQ, flat_rows.shape[1] // HDIM, HDIM)


def dot(a, b, dims):
    return lax.dot_general(a, b, (dims, ((), ())), preferred_element_type=F32)


def masked_scores(query_block, keys_all, valid_keys, score_scale):
    scores = jnp.einsum("sqhe,skhe->shqk", query_block, keys_all, preferred_element_type=F32) * score_scale
    return jnp.where(valid_keys[:, None, None, :], scores, NEG_LARGE)


def attention_forward(queries, keys_all, values_all, valid_keys, score_scale, block_rows):
    pieces = []
    log_sums = []
    for offset in range(0, SEQ, block_rows):
        scores = masked_scores(queries[:, offset : offset + block_rows], keys_all, valid_keys, score_scale)
        highest = jnp.max(scores, axis=-1, keepdims=True)
        weights = jnp.exp(scores - highest)
        totals = jnp.sum(weights, axis=-1, keepdims=True)
        softmax_low = (weights / totals).astype(BF16)
        mixture = jnp.einsum("shqk,skhe->sqhe", softmax_low, values_all, preferred_element_type=F32)
        pieces.append(mixture.astype(BF16))
        log_sums.append((highest + jnp.log(totals))[..., 0])
    return (jnp.concatenate(pieces, axis=1), jnp.concatenate(log_sums, axis=2))


def attention_backward(queries, keys_all, values_all, grad_attended, log_sums, valid_keys, score_scale, block_rows):
    grad_keys = jnp.zeros(keys_all.shape, F32)
    grad_values = jnp.zeros(values_all.shape, F32)
    grad_pieces = []
    for offset in range(0, SEQ, block_rows):
        query_block = queries[:, offset : offset + block_rows]
        grad_block = grad_attended[:, offset : offset + block_rows]
        scores = masked_scores(query_block, keys_all, valid_keys, score_scale)
        softmax_rows = jnp.exp(scores - log_sums[:, :, offset : offset + block_rows, None])
        grad_probs = jnp.einsum("sqhe,skhe->shqk", grad_block, values_all, preferred_element_type=F32)
        centre = jnp.sum(softmax_rows * grad_probs, axis=-1, keepdims=True)
        grad_scores = (softmax_rows * (grad_probs - centre)).astype(BF16)
        grad_pieces.append(
            jnp.einsum("shqk,skhe->sqhe", grad_scores, keys_all, preferred_element_type=F32) * score_scale
        )
        grad_keys = (
            grad_keys + jnp.einsum("shqk,sqhe->skhe", grad_scores, query_block, preferred_element_type=F32) * score_scale
        )
        grad_values = grad_values + jnp.einsum(
            "shqk,sqhe->skhe", softmax_rows.astype(BF16), grad_block, preferred_element_type=F32
        )
    return (jnp.concatenate(grad_pieces, axis=1), grad_keys, grad_values)


def body(
    dp_count,
    frames,
    cotangent,
    ada_gain,
    ada_shift,
    w_query,
    b_query,
    w_key,
    w_value,
    b_value,
    w_out,
    b_out,
    w_inner,
    b_inner,
    w_outer,
    b_outer,
    section_index,
    lengths,
    key_mask,
):
    rows_dev, width = frames.shape
    sections = ada_gain.shape[0]
    assert section_index.shape[0] == 1
    score_scale = HDIM ** (-0.5)
    block_rows = 512
    section = section_index[0] - 2
    gain = lax.dynamic_slice(ada_gain, (section, 0), (1, 2 * width))
    shift = lax.dynamic_slice(ada_shift, (section, 0), (1, 2 * width))
    pick = jnp.broadcast_to(
        (section == jnp.arange(sections, dtype=jnp.int32)).astype(F32)[:, None], (sections, 128)
    )
    spots = jnp.arange(SEQ, dtype=jnp.int32)
    valid_keys = (spots[None, :] < lengths[:, None]) & (key_mask.reshape(1, SEQ) > 0)
    inputs = frames.astype(F32)
    normed_one, inverse_one = normalize(inputs)
    first_low = (normed_one * gain[:, :width] + shift[:, :width]).astype(BF16)
    first_all = tensor_gather(first_low, 1)
    queries = (dot(first_all, w_query, ((1,), (0,))) + b_query).astype(BF16)
    keys_all = dot(first_all, w_key, ((1,), (0,))).astype(BF16)
    values_all = (dot(first_all, w_value, ((1,), (0,))) + b_value).astype(BF16)
    attended_heads, log_sums = attention_forward(
        split_heads(queries), split_heads(keys_all), split_heads(values_all), valid_keys, score_scale, block_rows
    )
    attended = attended_heads.reshape(queries.shape)
    hidden = inputs + tensor_scatter(dot(attended, w_out, ((1,), (0,))).astype(BF16), 2) + b_out
    normed_two, inverse_two = normalize(hidden)
    second_low = (normed_two * gain[:, width:] + shift[:, width:]).astype(BF16)
    second_all = tensor_gather(second_low, 3)
    grad_all = tensor_gather(cotangent, 4)
    inner_pre = dot(second_all, w_inner, ((1,), (0,))) + b_inner
    activated = exact_gelu(inner_pre).astype(BF16)
    layer_out = (
        hidden + tensor_scatter(dot(activated, w_outer, ((1,), (0,))).astype(BF16), 5) + b_outer
    ).astype(BF16)
    grad_w_outer = dot(activated, grad_all, ((0,), (0,))).astype(BF16)
    grad_activated = dot(grad_all, w_outer, ((1,), (1,)))
    unused_value, gelu_pull = jax.vjp(exact_gelu, inner_pre)
    grad_inner = gelu_pull(grad_activated)[0].astype(BF16)
    grad_w_inner = dot(second_all, grad_inner, ((0,), (0,))).astype(BF16)
    grad_b_inner = jnp.sum(grad_inner.astype(F32), axis=0)
    grad_second = tensor_scatter(dot(grad_inner, w_inner, ((1,), (1,))).astype(BF16), 6)
    grad_out_rows = cotangent.astype(F32)
    grad_hidden = grad_out_rows + norm_back(grad_second * gain[:, width:], normed_two, inverse_two)
    grad_attn_all = tensor_gather(grad_hidden.astype(BF16), 7)
    grad_w_out = dot(grad_attn_all, attended, ((0,), (0,)))
    grad_attended = dot(grad_attn_all, w_out, ((1,), (1,))).astype(BF16)
    grad_q_heads, grad_k_heads, grad_v_heads = attention_backward(
        split_heads(queries),
        split_heads(keys_all),
        split_heads(values_all),
        split_heads(grad_attended),
        log_sums,
        valid_keys,
        score_scale,
        block_rows,
    )
    grad_queries = grad_q_heads.reshape(queries.shape).astype(BF16)
    grad_keys = grad_k_heads.reshape(queries.shape).astype(BF16)
    grad_values = grad_v_heads.reshape(queries.shape).astype(BF16)
    grad_b_query = jnp.sum(grad_queries.astype(F32), axis=0)
    grad_b_value = jnp.sum(grad_values.astype(F32), axis=0)
    total_rows = dot(grad_queries, w_query, ((1,), (1,)))
    total_rows = total_rows + dot(grad_keys, w_key, ((1,), (1,)))
    total_rows = total_rows + dot(grad_values, w_value, ((1,), (1,)))
    grad_first = tensor_scatter(total_rows.astype(BF16), 8)
    grad_w_attn = jnp.concatenate(
        [
            dot(first_all, grad_queries, ((0,), (0,))).astype(BF16),
            dot(first_all, grad_keys, ((0,), (0,))).astype(BF16),
            dot(first_all, grad_values, ((0,), (0,))).astype(BF16),
            grad_w_out.astype(BF16),
        ],
        axis=1,
    )
    frames_grad = grad_hidden + norm_back(grad_first * gain[:, :width], normed_one, inverse_one)
    vec = jnp.concatenate(
        [
            jnp.sum(grad_first * normed_one, axis=0),
            jnp.sum(grad_second * normed_two, axis=0),
            jnp.sum(grad_first, axis=0),
            jnp.sum(grad_second, axis=0),
            jnp.sum(grad_hidden, axis=0),
            jnp.sum(grad_out_rows, axis=0),
        ]
    ).reshape(-1, 128)
    bias = jnp.concatenate(
        [grad_b_inner, grad_b_query, grad_b_value, jnp.zeros((2048 - 1024 - 512,), F32)]
    ).reshape(16, 128)
    sum_inner, sum_outer, sum_attn, small = dp_sum(
        dp_count, [grad_w_inner, grad_w_outer, grad_w_attn], [512, 512, 512], vec, bias, pick, 9
    )
    small = small.astype(F32)
    tables = small[: 32 * sections].reshape(sections, 2, 2 * width)
    shared = small[32 * sections : 32 * sections + 16].reshape(2, width)
    biases = small[32 * sections + 16 : 32 * sections + 32].reshape(-1)
    heads = w_query.shape[1]
    units = w_inner.shape[1]
    return (
        layer_out,
        frames_grad,
        tables[:, 0],
        tables[:, 1],
        sum_attn[:, :heads].astype(F32),
        biases[units : units + heads],
        sum_attn[:, heads : 2 * heads].astype(F32),
        sum_attn[:, 2 * heads : 3 * heads].astype(F32),
        biases[units + heads : units + 2 * heads],
        sum_attn[:, 3 * heads :].T.astype(F32),
        shared[0],
        sum_inner.astype(F32),
        biases[:units],
        sum_outer.astype(F32),
        shared[1],
    )


def solution(mesh):
    return jax.shard_map(
        functools.partial(body, mesh.shape["dp"]),
        mesh=mesh,
        in_specs=(
            P(("dp", "tensor"), None),
            P(("dp", "tensor"), None),
            P(),
            P(),
            P(None, "tensor"),
            P("tensor"),
            P(None, "tensor"),
            P(None, "tensor"),
            P("tensor"),
            P("tensor", None),
            P(),
            P(None, "tensor"),
            P("tensor"),
            P("tensor", None),
            P(),
            P("dp"),
            P("dp"),
            P("dp"),
        ),
        out_specs=(
            P(("dp", "tensor"), None),
            P(("dp", "tensor"), None),
            P(),
            P(),
            P(None, "tensor"),
            P("tensor"),
            P(None, "tensor"),
            P(None, "tensor"),
            P("tensor"),
            P("tensor", None),
            P(),
            P(None, "tensor"),
            P("tensor"),
            P("tensor", None),
            P(),
        ),
        check_vma=False,
    )
```

time: 923 us -> 460 us (0.50)
  waiting for transfers between devices: 714 us -> 0 us
  Pallas kernels: 0 us -> 297 us
  blocking collectives: 22.4 us -> 0 us
  between operations: 16.8 us -> 3.58 us
  local copies, waits for them, and re-layouts: 23.4 us -> 10.5 us
  other arithmetic: 36.3 us -> 46.7 us
    psum x2 -> x0, waiting for transfers between devices: 501 us -> none  [the longest x1 405 us: body(): lax.psum((grad_w_query, grad_b_query, grad_w_key, grad_w_value, grad_b_va...]
    pallas_call x0 -> x9, Pallas kernels: none -> 297 us  [the longest x1 153 us: dp_sum(): pl.pallas_call(functools.partial(dp_sum_kernel, count, tuple(widths)), ou...]
    reduce_scatter x4 -> x0, waiting for transfers between devices: 127 us -> none  [the longest x1 44.7 us: body(): lax.psum_scatter(jnp.dot(attended, w_out, preferred_element_type=jnp.floa...]
    all_gather x4 -> x0, waiting for transfers between devices: 86 us -> none  [the longest x1 24.3 us: body(): first_all = lax.all_gather(first_low, 'tensor', axis=0, tiled=True)]
    psum x1 -> x0, blocking collectives: 22.4 us -> none  [body(): lax.psum((grad_w_query, grad_b_query, grad_w_key, grad_w_value, grad_b_va...]
    unnamed x142 -> x126, local copies, waits for them, and re-layouts: 23.3 us -> 5.47 us
    dot_general x24 -> x20, matrix products: 77.5 us -> 63.6 us  [the longest x18 56.5 us: dot(): return lax.dot_general(a, b, (dims, ((), ())), preferred_element_type=F32)]
    convert_element_type x6 -> x10, other arithmetic: 17.3 us -> 25 us  [the longest x1 9.01 us: attention_backward(): grad_scores = (softmax_rows * (grad_probs - centre)).astype(BF16)]
  transfers between devices with their start and end apart: 10 -> 0, of which waited for: 10 -> 0; matrix products, arithmetic and copies ran while one was open for 4% -> 0% of each run, Pallas kernels for 0% -> 0%
where the time goes in v1:
time: 460 us; the launch traced here: 454 us
  Pallas kernels  297 us (65%)
  matrix products  96 us (21%)
  other arithmetic  46.7 us (10%)
  local copies, waits for them, and re-layouts  10.5 us (2%)
    pallas_call x1, Pallas kernels, dp_sum(): pl.pallas_call(functools.partial(dp_sum_kernel, count, tuple(widths)), ou...  153 us
    pallas_call x4, Pallas kernels, tensor_scatter(): pl.pallas_call(scatter_kernel, out_shape=jax.ShapeDtypeStruct((rows, widt...  72.9 us
    pallas_call x4, Pallas kernels, tensor_gather(): pl.pallas_call(gather_kernel, out_shape=jax.ShapeDtypeStruct((rows * 4, w...  71.6 us
    dot_general x18, matrix products, dot(): return lax.dot_general(a, b, (dims, ((), ())), preferred_element_type=F32)  56.5 us
    dot_general x2, matrix products, attention_backward(): jnp.einsum('sqhe,skhe->shqk', grad_block, values_all, preferred_element_t...  19.3 us

profile of v1, /device:TPU:0, one launch (start us, length us, event | category | flops | bytes accessed | tf_op | source)
XLA Modules:
  0.0 453.9 jit_solution(11023960706985029107)
XLA Ops:
  2.9 1.2 convert_reduce_fusion.1
  4.1 1.3 fusion.49
  6.1 1.5 fusion.70
  8.2 2.1 fusion.43.x_ref
  10.3 19.1 %tensor_gather_1.1 = bf16[1024,1024]{1,0:T(8,128)(2,1)} custom-call(bf16[256,1024]{1,0:T(8,128)(2,1)} %fusion.43.x_ref), custom_call_target="tpu_custom_call" | custom-call | tf_op jit(solution)/shard_map/tensor_gather_1/pallas_call | solution.py:79
  29.4 2.5 convolution_convert_fusion.10
  31.9 2.5 fusion.29
  35.3 17.9 %tensor_gather_4.1 = bf16[1024,1024]{1,0:T(8,128)(2,1)} custom-call(bf16[256,1024]{1,0:T(8,128)(2,1)} %x_ref.1), custom_call_target="tpu_custom_call" | custom-call | tf_op jit(solution)/shard_map/tensor_gather_4/pallas_call | solution.py:79
  53.2 1.3 fusion.53
  54.5 2.3 fusion.18
  56.9 4.3 fusion
  61.2 2.5 fusion.41
  63.8 2.5 fusion.40
  67.1 2.1 convolution_convert_fusion.4.p_ref
  69.2 18.3 %tensor_scatter_2.1 = f32[256,1024]{1,0:T(8,128)} custom-call(bf16[1024,1024]{1,0:T(8,128)(2,1)} %convolution_convert_fusion.4.p_ref), custom_call_target="tpu_custom_call" | custom-call | tf_op jit(solution)/shard_map/tensor_scatter_2/pallas_call | solution.py:131
  87.6 1.5 fusion.67
  90.4 17.2 %tensor_gather_3.1 = bf16[1024,1024]{1,0:T(8,128)(2,1)} custom-call(bf16[256,1024]{1,0:T(8,128)(2,1)} %add_convert_fusion.3.x_ref), custom_call_target="tpu_custom_call" | custom-call | tf_op jit(solution)/shard_map/tensor_gather_3/pallas_call | solution.py:79
  107.6 4.7 %fusion.72 = f32[1024,1024]{1,0:T(8,128)S(1)} fusion(bf16[1024,1024]{1,0:T(8,128)(2,1)} %tensor_gather_3.1, bf16[1024,1024]{1,0:T(8,128)(2,1)} %param.29), kind=kOutput, calls=%fused_computation.159 | convolution fusion | flops 2147483648 | bytes 8388608 | tf_op jit(solution)/shard_map/dot_general | solution.py:443
  112.3 12.6 %convert_reduce_fusion = (f32[1024]{0:T(1024)}, bf16[1024,1024]{1,0:T(8,128)(2,1)S(1)}, f32[1024,1024]{1,0:T(8,128)S(1)}) fusion(f32[1024,1024]{1,0:T(8,128)S(1)} %fusion.72, f32[1024]{0:T(1024)S(1)} %copy-done.46, bf16[1024,1024]{1,0:T(8,128)(2,1)S(1)} %copy-done.15, bf16[1024,1024]{1,0:T(8,128)(2,1)S(1)} %copy-done), kind=kOutput, calls=%fused_computation.20 | convolution fusion | flops 2226125824 | bytes 14688256 | tf_op jit(solution)/shard_map/dot_general | solution.py:443
  124.9 3.8 convolution_convert_fusion.1.refs_0_
  129.8 3.8 convolution_convert_fusion.refs_1_
  133.7 3.7 convolution_convert_fusion.3.p_ref
  137.3 18.3 %tensor_scatter_5.1 = f32[256,1024]{1,0:T(8,128)} custom-call(bf16[1024,1024]{1,0:T(8,128)(2,1)} %convolution_convert_fusion.3.p_ref), custom_call_target="tpu_custom_call" | custom-call | tf_op jit(solution)/shard_map/tensor_scatter_5/pallas_call | solution.py:131
  155.7 5.9 %convolution_convert_fusion.2.p_ref = bf16[1024,1024]{1,0:T(8,128)(2,1)} fusion(bf16[1024,1024]{1,0:T(8,128)(2,1)} %copy-done.52, bf16[1024,1024]{1,0:T(8,128)(2,1)} %param.29), kind=kOutput, calls=%fused_computation.46 | convolution fusion | flops 2148532224 | bytes 6291456 | tf_op jit(solution)/shard_map/dot_general | solution.py:443
  161.6 17.9 %tensor_scatter_6.1 = f32[256,1024]{1,0:T(8,128)} custom-call(bf16[1024,1024]{1,0:T(8,128)(2,1)} %convolution_convert_fusion.2.p_ref), custom_call_target="tpu_custom_call" | custom-call | tf_op jit(solution)/shard_map/tensor_scatter_6/pallas_call | solution.py:131
  179.5 2.3 multiply_reduce_fusion.2
  181.8 3.3 fusion.66
  186.0 17.5 %tensor_gather_7.1 = bf16[1024,1024]{1,0:T(8,128)(2,1)} custom-call(bf16[256,1024]{1,0:T(8,128)(2,1)} %convert_element_type.219.x_ref), custom_call_target="tpu_custom_call" | custom-call | tf_op jit(solution)/shard_map/tensor_gather_7/pallas_call | solution.py:79
  203.5 3.5 convolution_convert_fusion.5
  207.8 4.9 %fusion.5 = f32[4,64,1024]{2,1,0:T(8,128)S(1)} fusion(f32[4,512]{1,0:T(4,128)S(1)} %log_add_fusion, f32[4,512,1024]{2,1,0:T(8,128)} %copy-done.2, pred[1024]{0:T(1024)(128)(4,1)S(1)} %fusion.56, bf16[1,1024,4,64]{1,3,2,0:T(8,128)(2,1)S(1)} %bitcast.166), kind=kOutput, calls=%fused_computation.18 | convolution fusion | flops 276824064 | bytes 9708544 | tf_op jit(solution)/shard_map/shqk,sqhe->skhe/dot_general | solution.py:484
  213.2 2.2 convert_reduce_fusion.3
  216.2 3.2 convolution_convert_fusion.6
  219.3 5.5 %fusion.55 = f32[4,512,1024]{2,1,0:T(8,128)} fusion(bf16[1024,4,64]{0,2,1:T(8,128)(2,1)S(1)} %bitcast.160, bf16[1,1024,4,64]{1,3,2,0:T(8,128)(2,1)S(1)} %bitcast.168), kind=kOutput, calls=%fused_computation.116 | convolution fusion | flops 268435456 | bytes 9175040 | tf_op jit(solution)/shard_map/sqhe,skhe->shqk/dot_general | solution.py:475
  224.8 13.8 %multiply_reduce_fusion.1 = (f32[4,512]{1,0:T(4,128)S(1)}, f32[4,512]{1,0:T(4,128)}, f32[4,512,1024]{2,1,0:T(8,128)}) fusion(f32[4,512]{1,0:T(4,128)S(1)} %log_add_fusion.1, f32[4,512,1024]{2,1,0:T(8,128)} %copy-done.3, pred[1024]{0:T(1024)(128)(4,1)} %copy-done.35, f32[4,512,1024]{2,1,0:T(8,128)} %fusion.55, f32[4,512]{1,0:T(4,128)S(1)} %log_add_fusion, ...), kind=kOutput, calls=%fused_computation.4 | convolution fusion | flops 289402880 | bytes 34374656 | tf_op jit(solution)/shard_map/sqhe,skhe->shqk/dot_general | solution.py:475
  238.6 9.0 %multiply_convert_fusion.1 = (bf16[4,512,1024]{2,1,0:T(8,128)(2,1)S(1)}, bf16[4,512,1024]{2,1,0:T(8,128)(2,1)S(1)}) fusion(f32[4,512,1024]{2,1,0:T(8,128)} %get-tuple-element.81, f32[4,512]{1,0:T(4,128)S(1)} %get-tuple-element.46, f32[4,512]{1,0:T(4,128)S(1)} %log_add_fusion.1, f32[4,512,1024]{2,1,0:T(8,128)S(1)} %bitcast.147, pred[1024]{0:T(1024)(128)(4,1)} %copy-done.35, ...), kind=kLoop, calls=%fused_computation.3 | loop fusion | flops 25165824 | bytes 41976832 | tf_op jit(solution)/shard_map/convert_element_type | solution.py:477
  247.7 1.4 fusion.36
  250.8 1.4 fusion.37
  253.1 2.4 convolution_convert_fusion.8
  256.4 1.6 pad_maximum_fusion.refs_2_
  259.6 2.1 add_convert_fusion.p_ref
  261.7 18.3 %tensor_scatter_8.1 = f32[256,1024]{1,0:T(8,128)} custom-call(bf16[1024,1024]{1,0:T(8,128)(2,1)} %add_convert_fusion.p_ref), custom_call_target="tpu_custom_call" | custom-call | tf_op jit(solution)/shard_map/tensor_scatter_8/pallas_call | solution.py:131
  280.1 1.8 fusion.48
  281.8 2.6 fusion.47
  285.1 152.7 %dp_sum.1 = (bf16[1024,1024]{1,0:T(8,128)(2,1)}, bf16[1024,1024]{1,0:T(8,128)(2,1)}, bf16[1024,1024]{1,0:T(8,128)(2,1)}, bf16[256,128]{1,0:T(8,128)(2,1)}) custom-call(bf16[1024,1024]{1,0:T(8,128)(2,1)} %convolution_convert_fusion.1.refs_0_, bf16[1024,1024]{1,0:T(8,128)(2,1)} %convolution_convert_fusion.refs_1_, bf16[1024,1024]{1,0:T(8,128)(2,1)} %pad_maximum_fusion.refs_2_, ...), custom_call_target="tpu_custom_call" | custom-call | tf_op jit(solution)/shard_map/dp_sum/pallas_call | solution.py:408
  442.1 3.3 convert_bitcast_fusion
  445.4 1.3 copy.39
  446.7 4.2 convert_element_type.252
  451.0 2.5 convert_element_type.253
  (165 shorter events, 19.0 us)
Async XLA Ops:
  0.6 111.6 %copy-start = (bf16[1024,1024]{1,0:T(8,128)(2,1)S(1)}, bf16[1024,1024]{1,0:T(8,128)(2,1)}, u32[]{:S(2)}) copy-start(bf16[1024,1024]{1,0:T(8,128)(2,1)} %param.31) | copy-start | bytes 6291460
  0.7 28.7 %copy-start.20 = (bf16[1024,256]{1,0:T(8,128)(2,1)S(1)}, bf16[1024,256]{1,0:T(8,128)(2,1)}, u32[]{:S(2)}) copy-start(bf16[1024,256]{1,0:T(8,128)(2,1)} %param.24) | copy-start | bytes 1572868
  0.7 31.2 %copy-start.22 = (bf16[1024,256]{1,0:T(8,128)(2,1)S(1)}, bf16[1024,256]{1,0:T(8,128)(2,1)}, u32[]{:S(2)}) copy-start(bf16[1024,256]{1,0:T(8,128)(2,1)} %param.22) | copy-start | bytes 1572868
  0.7 31.2 %copy-start.50 = (f32[256]{0:T(256)S(1)}, f32[256]{0:T(256)}, u32[]{:S(2)}) copy-start(f32[256]{0:T(256)} %param.23) | copy-start | bytes 3076
  2.9 209.8 %copy-start.35 = (pred[1024]{0:T(1024)(128)(4,1)}, pred[1024]{0:T(1024)(128)(4,1)S(1)}, u32[]{:S(2)}) copy-start(pred[1024]{0:T(1024)(128)(4,1)S(1)} %fusion.56) | copy-start | bytes 3076
  4.1 30.4 %copy-start.36 = (f32[256]{0:T(256)}, f32[256]{0:T(256)S(1)}, u32[]{:S(2)}) copy-start(f32[256]{0:T(256)S(1)} %broadcast_multiply_fusion.5) | copy-start | bytes 3076
  5.5 29.0 %copy-start.41 = (f32[256]{0:T(256)}, f32[256]{0:T(256)S(1)}, u32[]{:S(2)}) copy-start(f32[256]{0:T(256)S(1)} %add_rsqrt_fusion.1) | copy-start | bytes 3076
  29.4 5.1 %copy-start.13 = (bf16[1024,1024]{1,0:T(8,128)(2,1)S(1)}, bf16[1024,1024]{1,0:T(8,128)(2,1)}, u32[]{:S(2)}) copy-start(bf16[1024,1024]{1,0:T(8,128)(2,1)} %tensor_gather_1.1) | copy-start | bytes 6291460
  29.4 5.1 %copy-start.24 = (bf16[1024,256]{1,0:T(8,128)(2,1)S(1)}, bf16[1024,256]{1,0:T(8,128)(2,1)}, u32[]{:S(2)}) copy-start(bf16[1024,256]{1,0:T(8,128)(2,1)} %param.25) | copy-start | bytes 1572868
  29.4 5.1 %copy-start.51 = (f32[256]{0:T(256)S(1)}, f32[256]{0:T(256)}, u32[]{:S(2)}) copy-start(f32[256]{0:T(256)} %param.26) | copy-start | bytes 3076
  31.9 22.6 %copy-start.5 = (bf16[1024,256]{0,1:T(8,128)(2,1)}, bf16[1024,256]{0,1:T(8,128)(2,1)S(1)}, u32[]{:S(2)}) copy-start(bf16[1024,256]{0,1:T(8,128)(2,1)S(1)} %convolution_convert_fusion.10) | copy-start | bytes 1572868
  34.5 20.0 %copy-start.8 = (bf16[1024,256]{0,1:T(8,128)(2,1)}, bf16[1024,256]{0,1:T(8,128)(2,1)S(1)}, u32[]{:S(2)}) copy-start(bf16[1024,256]{0,1:T(8,128)(2,1)S(1)} %fusion.29) | copy-start | bytes 1572868
  35.3 28.4 %copy-start.10 = (bf16[1024,256]{0,1:T(8,128)(2,1)}, bf16[1024,256]{0,1:T(8,128)(2,1)S(1)}, u32[]{:S(2)}) copy-start(bf16[1024,256]{0,1:T(8,128)(2,1)S(1)} %fusion.28) | copy-start | bytes 1572868
  54.5 6.7 %copy-start.2 = (f32[4,512,1024]{2,1,0:T(8,128)}, f32[4,512,1024]{2,1,0:T(8,128)S(1)}, u32[]{:S(2)}) copy-start(f32[4,512,1024]{2,1,0:T(8,128)S(1)} %fusion.53) | copy-start | bytes 25165828
  56.8 6.9 %copy-start.3 = (f32[4,512,1024]{2,1,0:T(8,128)}, f32[4,512,1024]{2,1,0:T(8,128)S(1)}, u32[]{:S(2)}) copy-start(f32[4,512,1024]{2,1,0:T(8,128)S(1)} %get-tuple-element.80) | copy-start | bytes 25165828
  63.8 3.4 copy-start.28
  66.3 21.3 %copy-start.4 = (bf16[256,1024]{1,0:T(8,128)(2,1)S(1)}, bf16[256,1024]{1,0:T(8,128)(2,1)}, u32[]{:S(2)}) copy-start(bf16[256,1024]{1,0:T(8,128)(2,1)} %param.18) | copy-start | bytes 1572868
  66.3 21.3 %copy-start.45 = (f32[1024]{0:T(1024)S(1)}, f32[1024]{0:T(1024)}, u32[]{:S(2)}) copy-start(f32[1024]{0:T(1024)} %param.28) | copy-start | bytes 12292
  69.2 20.1 %copy-start.38 = (f32[1,1024]{1,0:T(1,128)S(1)}, f32[1,1024]{1,0:T(1,128)}, u32[]{:S(2)}) copy-start(f32[1,1024]{1,0:T(1,128)} %get-tuple-element.85) | copy-start | bytes 12292
  107.6 4.7 %copy-start.15 = (bf16[1024,1024]{1,0:T(8,128)(2,1)S(1)}, bf16[1024,1024]{1,0:T(8,128)(2,1)}, u32[]{:S(2)}) copy-start(bf16[1024,1024]{1,0:T(8,128)(2,1)} %tensor_gather_4.1) | copy-start | bytes 6291460
  107.6 4.7 %copy-start.46 = (f32[1024]{0:T(1024)S(1)}, f32[1024]{0:T(1024)}, u32[]{:S(2)}) copy-start(f32[1024]{0:T(1024)} %param.30) | copy-start | bytes 12292
  112.3 12.6 %copy-start.16 = (bf16[1024,1024]{1,0:T(8,128)(2,1)S(1)}, bf16[1024,1024]{1,0:T(8,128)(2,1)}, u32[]{:S(2)}) copy-start(bf16[1024,1024]{1,0:T(8,128)(2,1)} %tensor_gather_3.1) | copy-start | bytes 6291460
  124.9 3.8 copy-start.52
  161.6 20.2 %copy-start.7 = (f32[256,1024]{1,0:T(8,128)S(1)}, f32[256,1024]{1,0:T(8,128)}, u32[]{:S(2)}) copy-start(f32[256,1024]{1,0:T(8,128)} %tensor_scatter_5.1) | copy-start | bytes 3145732
  161.6 20.2 %copy-start.49 = (f32[1024]{0:T(1024)S(1)}, f32[1024]{0:T(1024)}, u32[]{:S(2)}) copy-start(f32[1024]{0:T(1024)} %param.32) | copy-start | bytes 12292
  185.1 18.4 %copy-start.19 = (bf16[1,1024,4,64]{1,3,2,0:T(8,128)(2,1)S(1)}, bf16[1,1024,4,64]{1,3,2,0:T(8,128)(2,1)}, u32[]{:S(2)}) copy-start(bf16[1,1024,4,64]{1,3,2,0:T(8,128)(2,1)} %copy-done.18) | copy-start | bytes 1572868
  186.0 21.1 %copy-start.29 = (bf16[256,1024]{1,0:T(8,128)(2,1)S(1)}, bf16[256,1024]{1,0:T(8,128)(2,1)}, u32[]{:S(2)}) copy-start(bf16[256,1024]{1,0:T(8,128)(2,1)} %param.27) | copy-start | bytes 1572868
  203.5 3.5 copy-start.17
  207.0 5.6 %slice-start.2 = ((s8[8388608]{0:T(1024)(128)(4,1)}), s8[4194304]{0:T(1024)(128)(4,1)S(1)}, s32[]{:S(2)}) async-start(s8[8388608]{0:T(1024)(128)(4,1)} %bitcast.144), calls=%async_computation.2 | async-start | bytes 8388608
  207.8 5.4 %slice-start.3 = ((s8[8388608]{0:T(1024)(128)(4,1)}), s8[4194304]{0:T(1024)(128)(4,1)S(1)}, s32[]{:S(2)}) async-start(s8[8388608]{0:T(1024)(128)(4,1)} %bitcast.144), calls=%async_computation.3 | async-start | bytes 8388608
  215.4 3.9 copy-start.11
  219.3 19.3 %slice-start = ((s8[8388608]{0:T(1024)(128)(4,1)}), s8[4194304]{0:T(1024)(128)(4,1)S(1)}, s32[]{:S(2)}) async-start(s8[8388608]{0:T(1024)(128)(4,1)} %bitcast.142), calls=%async_computation | async-start | bytes 8388608
  219.3 19.3 %slice-start.4 = ((s8[8388608]{0:T(1024)(128)(4,1)}), s8[4194304]{0:T(1024)(128)(4,1)S(1)}, s32[]{:S(2)}) async-start(s8[8388608]{0:T(1024)(128)(4,1)} %bitcast.146), calls=%async_computation.4 | async-start | bytes 8388608
  224.8 13.8 %slice-start.1 = ((s8[8388608]{0:T(1024)(128)(4,1)}), s8[4194304]{0:T(1024)(128)(4,1)S(1)}, s32[]{:S(2)}) async-start(s8[8388608]{0:T(1024)(128)(4,1)} %bitcast.142), calls=%async_computation.1 | async-start | bytes 8388608
  224.8 13.8 %slice-start.5 = ((s8[8388608]{0:T(1024)(128)(4,1)}), s8[4194304]{0:T(1024)(128)(4,1)S(1)}, s32[]{:S(2)}) async-start(s8[8388608]{0:T(1024)(128)(4,1)} %bitcast.146), calls=%async_computation.5 | async-start | bytes 8388608
  238.6 9.0 %copy-start.6 = (bf16[1024,256]{0,1:T(8,128)(2,1)S(1)}, bf16[1024,256]{0,1:T(8,128)(2,1)}, u32[]{:S(2)}) copy-start(bf16[1024,256]{0,1:T(8,128)(2,1)} %copy-done.5) | copy-start | bytes 1572868
  252.5 3.1 copy-start.14
  253.1 3.2 copy-start.30
  253.1 3.3 copy-start.31
  259.6 20.5 %copy-start.33 = (f32[1,1024]{1,0:T(1,128)S(1)}, f32[1,1024]{1,0:T(1,128)}, u32[]{:S(2)}) copy-start(f32[1,1024]{1,0:T(1,128)} %copy-done.32) | copy-start | bytes 12292
  259.6 20.5 %copy-start.37 = (f32[256]{0:T(256)S(1)}, f32[256]{0:T(256)}, u32[]{:S(2)}) copy-start(f32[256]{0:T(256)} %copy-done.36) | copy-start | bytes 3076
  259.6 20.5 %copy-start.42 = (f32[256]{0:T(256)S(1)}, f32[256]{0:T(256)}, u32[]{:S(2)}) copy-start(f32[256]{0:T(256)} %copy-done.41) | copy-start | bytes 3076
  261.7 22.8 %copy-start.40 = (f32[1024]{0:T(1024)S(1)}, f32[1024]{0:T(1024)}, u32[]{:S(2)}) copy-start(f32[1024]{0:T(1024)} %get-tuple-element.38) | copy-start | bytes 12292
  261.7 22.8 %copy-start.39 = (f32[1024]{0:T(1024)S(1)}, f32[1024]{0:T(1024)}, u32[]{:S(2)}) copy-start(f32[1024]{0:T(1024)} %get-tuple-element.44) | copy-start | bytes 12292
  261.7 22.8 %copy-start.44 = (f32[1024]{0:T(1024)S(1)}, f32[1024]{0:T(1024)}, u32[]{:S(2)}) copy-start(f32[1024]{0:T(1024)} %get-tuple-element.57) | copy-start | bytes 12292
  261.7 22.8 %copy-start.43 = (f32[1024]{0:T(1024)S(1)}, f32[1024]{0:T(1024)}, u32[]{:S(2)}) copy-start(f32[1024]{0:T(1024)} %get-tuple-element.66) | copy-start | bytes 12292
  446.7 4.2 copy-start.12
  446.7 6.7 %copy-start.1 = (bf16[1024,1024]{1,0:T(8,128)(2,1)S(1)}, bf16[1024,1024]{1,0:T(8,128)(2,1)}, u32[]{:S(2)}) copy-start(bf16[1024,1024]{1,0:T(8,128)(2,1)} %param.31) | copy-start | bytes 6291460
  (11 other events, 15.5 us)

commit v2 on v1

--- a/solution.py
+++ b/solution.py
@@ -417,6 +417,302 @@
     )(*grads, vec, bias, pick)
 
 
+class Turns:
+    def __init__(self, generators):
+        self.waiting = list(generators)
+        self.running = []
+        for generator in self.waiting:
+            next(generator)
+
+    def turn(self):
+        if self.waiting:
+            self.running.append(self.waiting.pop(0))
+        still = []
+        for generator in self.running:
+            try:
+                next(generator)
+                still.append(generator)
+            except StopIteration:
+                pass
+        self.running = still
+
+    def drain(self):
+        while self.waiting or self.running:
+            self.turn()
+
+
+class Scatter:
+    def __init__(self, spot, p_ref, from_sib, chip_sum, landed, send, recv):
+        self.dp, self.me, self.sib, self.across, self.diag = spot
+        self.rows = p_ref.shape[0] // 4
+        self.part = self.rows // PARTS
+        self.p_ref, self.from_sib, self.chip_sum, self.landed = p_ref, from_sib, chip_sum, landed
+
+        def near(owner, which, i):
+            slot = which * PARTS + i
+            return remote(
+                p_ref.at[self.at(owner, i)],
+                from_sib.at[which, self.here(i)],
+                send.at[slot],
+                recv.at[slot],
+                (self.dp, self.sib),
+            )
+
+        self.first = [near(self.diag, 0, i) for i in range(PARTS)]
+        self.last = [near(self.sib, 1, i) for i in range(PARTS)]
+        self.crossing = [
+            remote(
+                chip_sum.at[self.here(i)],
+                landed.at[self.here(i)],
+                send.at[2 * PARTS + i],
+                recv.at[2 * PARTS + i],
+                (self.dp, self.across),
+            )
+            for i in range(PARTS)
+        ]
+
+    def here(self, i):
+        return pl.ds(i * self.part, self.part)
+
+    def at(self, owner, i):
+        return pl.ds(pl.multiple_of(owner * self.rows + i * self.part, self.part), self.part)
+
+    def start_first(self):
+        for copy in self.first:
+            copy.start()
+
+    def start_last(self):
+        for copy in self.last:
+            copy.start()
+
+    def cross(self):
+        for i in range(PARTS):
+            self.first[i].wait_recv()
+            self.chip_sum[self.here(i), :] = (
+                self.p_ref[self.at(self.across, i), :].astype(F32) + self.from_sib[0, self.here(i), :].astype(F32)
+            ).astype(BF16)
+            self.crossing[i].start()
+
+    def result(self, i):
+        self.last[i].wait_recv()
+        total = self.p_ref[self.at(self.me, i), :].astype(F32) + self.from_sib[1, self.here(i), :].astype(F32)
+        self.crossing[i].wait_recv()
+        return total + self.landed[self.here(i), :].astype(F32)
+
+    def finish(self):
+        for copy in self.first + self.last + self.crossing:
+            copy.wait_send()
+
+
+def late_kernel(count, width, *refs):
+    p_ref, normed_ref, inverse_ref, cot_ref, gain_ref, w_out_ref = refs[:6]
+    q_ref, k_ref, kt_ref, v_ref, log_ref, bias_ref = refs[6:12]
+    wq_ref, wk_ref, wv_ref, gi_ref, go_ref = refs[12:17]
+    gsec_ref, ghid_ref, gattn_ref, dq_ref, dk_ref, dv_ref, gfirst_ref, si_ref, so_ref = refs[17:26]
+    rest = refs[26:]
+    from_one, chip_one, landed_one, send_one, recv_one = rest[:5]
+    from_two, chip_two, landed_two, send_two, recv_two = rest[5:10]
+    total_ref, gsend, grecv = rest[10:13]
+    do_cat, q_cat, p_scr, ds_scr, dk_acc, dv_acc, dqt_ref = rest[13:20]
+    rest = rest[20:]
+    spot = places()
+    dp, me, sib, across, diag = spot
+    lines = lines_of(count, dp, me)
+    barrier = pltpu.get_barrier_semaphore()
+    for partner in [(dp, sib), (dp, across), lines[0].pair]:
+        pl.semaphore_signal(barrier, inc=1, device_id=partner, device_id_type=MESH)
+    waits = 3
+    for line in lines[1:]:
+        has_right = line.place < line.size - 1
+        has_left = line.place > 0
+        for partner, has in ((line.right, has_right), (line.left, has_left)):
+            pl.when(has)(
+                lambda partner=partner: pl.semaphore_signal(
+                    barrier, inc=1, device_id=partner, device_id_type=MESH
+                )
+            )
+        waits = waits + has_right.astype(jnp.int32) + has_left.astype(jnp.int32)
+    pl.semaphore_wait(barrier, waits)
+
+    rows = normed_ref.shape[0]
+    one = Scatter(spot, p_ref, from_one, chip_one, landed_one, send_one, recv_one)
+    one.start_first()
+    one.start_last()
+    per = 2 + 2 * (len(lines) - 1)
+    chunks = []
+    for x_ref, o_ref in ((gi_ref, si_ref), (go_ref, so_ref)):
+        for start in range(0, x_ref.shape[1], width):
+            chunks.append(
+                sum_chunk(lines, x_ref, o_ref, pl.ds(start, width), rest[:per], rest[per], rest[per + 1])
+            )
+            rest = rest[per + 2 :]
+    turns = Turns(chunks)
+    one.cross()
+
+    dk_acc[...] = jnp.zeros_like(dk_acc)
+    dv_acc[...] = jnp.zeros_like(dv_acc)
+    part = rows // PARTS
+    to_across, to_sib, passed = [], [], []
+
+    def block_part(owner, i):
+        return gattn_ref.at[pl.ds(pl.multiple_of(owner * rows + i * part, part), part)]
+
+    for i in range(PARTS):
+        here = pl.ds(i * part, part)
+        grad_second = one.result(i)
+        gsec_ref[here, :] = grad_second
+        normed = normed_ref[here, :]
+        grad_hat = grad_second * gain_ref[...]
+        back = inverse_ref[here, :] * (
+            grad_hat
+            - jnp.mean(grad_hat, axis=-1, keepdims=True)
+            - normed * jnp.mean(grad_hat * normed, axis=-1, keepdims=True)
+        )
+        grad_hidden = cot_ref[here, :].astype(F32) + back
+        ghid_ref[here, :] = grad_hidden
+        gattn_ref[pl.ds(pl.multiple_of(me * rows + i * part, part), part), :] = grad_hidden.astype(BF16)
+        ref = block_part(me, i)
+        to_across.append(remote(ref, ref, gsend.at[i], grecv.at[i], (dp, across)))
+        to_across[-1].start()
+        to_sib.append(remote(ref, ref, gsend.at[PARTS + i], grecv.at[PARTS + i], (dp, sib)))
+        to_sib[-1].start()
+    turns.turn()
+
+    heads = q_ref.shape[1] // HDIM
+    scale = HDIM ** (-0.5)
+    lanes = lax.broadcasted_iota(jnp.int32, (rows, q_ref.shape[1]), 1) // HDIM
+
+    def attend(owner):
+        block = pl.ds(pl.multiple_of(owner * rows, rows), rows)
+        grad_att = dot(gattn_ref[block, :], w_out_ref[...], ((1,), (1,))).astype(BF16)
+        query = q_ref[block, :]
+        for h in range(heads):
+            do_cat[pl.ds(h * rows, rows), :] = jnp.where(lanes == h, grad_att, jnp.zeros_like(grad_att))
+            q_cat[pl.ds(h * rows, rows), :] = jnp.where(lanes == h, query, jnp.zeros_like(query))
+
+        @pl.loop(0, heads)
+        def _(h):
+            at = pl.ds(pl.multiple_of(h * rows, rows), rows)
+            scores = dot(k_ref[...], q_cat[at, :], ((1,), (1,)))
+            probs = jnp.exp(scores * scale + (bias_ref[...] - log_ref[owner * heads + h]))
+            grad_probs = dot(v_ref[...], do_cat[at, :], ((1,), (1,)))
+            centre = jnp.sum(probs * grad_probs, axis=0, keepdims=True)
+            grad_scores = (probs * (grad_probs - centre)).astype(BF16)
+            p_scr[:, at] = probs.astype(BF16)
+            ds_scr[:, at] = grad_scores
+            head = pl.ds(pl.multiple_of(h * HDIM, HDIM), HDIM)
+            dqt_ref[owner, head, :] = dot(kt_ref[head, :], grad_scores, ((1,), (0,)))
+
+        dv_acc[...] += dot(p_scr[...], do_cat[...], ((1,), (0,)))
+        dk_acc[...] += dot(ds_scr[...], q_cat[...], ((1,), (0,)))
+
+    def pass_on(i):
+        to_across[i].wait_recv()
+        ref = block_part(across, i)
+        passed.append(remote(ref, ref, gsend.at[2 * PARTS + i], grecv.at[2 * PARTS + i], (dp, sib)))
+        passed[-1].start()
+
+    attend(me)
+    turns.turn()
+    pass_on(0)
+    pass_on(1)
+    for copy in to_sib:
+        copy.wait_recv()
+    attend(sib)
+    pass_on(2)
+    pass_on(3)
+    turns.turn()
+    attend(across)
+    turns.turn()
+    for copy in passed:
+        copy.wait_recv()
+    attend(diag)
+    turns.turn()
+
+    dk_ref[...] = (dk_acc[...] * scale).astype(BF16)
+    dv_ref[...] = dv_acc[...].astype(BF16)
+    two = Scatter(spot, total_ref, from_two, chip_two, landed_two, send_two, recv_two)
+
+    def total(owner):
+        block = pl.ds(pl.multiple_of(owner * rows, rows), rows)
+        grad_query = (dqt_ref[owner].T * scale).astype(BF16)
+        dq_ref[block, :] = grad_query
+        total_ref[block, :] = (
+            dot(grad_query, wq_ref[...], ((1,), (1,)))
+            + dot(dk_ref[block, :], wk_ref[...], ((1,), (1,)))
+            + dot(dv_ref[block, :], wv_ref[...], ((1,), (1,)))
+        ).astype(BF16)
+
+    total(diag)
+    two.start_first()
+    total(across)
+    two.cross()
+    total(sib)
+    two.start_last()
+    total(me)
+    turns.turn()
+    for i in range(PARTS):
+        gfirst_ref[pl.ds(i * part, part), :] = two.result(i)
+    turns.drain()
+    one.finish()
+    two.finish()
+    for copy in to_across + to_sib + passed:
+        copy.wait_send()
+
+
+def late(count, width, cid, *operands):
+    normed, q, gi, go = operands[1], operands[6], operands[15], operands[16]
+    rows, model = normed.shape
+    seq, local = q.shape
+    heads = local // HDIM
+    sems = chunk_sems(count)
+
+    def dma(n):
+        return [pltpu.SemaphoreType.DMA((n,))] * 2
+
+    def scatter_scratch():
+        return [
+            pltpu.VMEM((2, rows, model), BF16),
+            pltpu.VMEM((rows, model), BF16),
+            pltpu.VMEM((rows, model), BF16),
+        ] + dma(3 * PARTS)
+
+    scratch = scatter_scratch() + scatter_scratch()
+    scratch += [pltpu.VMEM((seq, model), BF16)] + dma(3 * PARTS)
+    scratch += [
+        pltpu.VMEM((heads * rows, local), BF16),
+        pltpu.VMEM((heads * rows, local), BF16),
+        pltpu.VMEM((seq, heads * rows), BF16),
+        pltpu.VMEM((seq, heads * rows), BF16),
+        pltpu.VMEM((seq, local), F32),
+        pltpu.VMEM((seq, local), F32),
+        pltpu.VMEM((seq // rows, local, rows), F32),
+    ]
+    for grad in (gi, go):
+        for _ in range(0, grad.shape[1], width):
+            scratch += chunk_scratch(count, grad.shape[0], width) + dma(sems)
+    shape = jax.ShapeDtypeStruct
+    return pl.pallas_call(
+        functools.partial(late_kernel, count, width),
+        out_shape=[
+            shape((rows, model), F32),
+            shape((rows, model), F32),
+            shape((seq, model), BF16),
+            shape((seq, local), BF16),
+            shape((seq, local), BF16),
+            shape((seq, local), BF16),
+            shape((rows, model), F32),
+            shape(gi.shape, BF16),
+            shape(go.shape, BF16),
+        ],
+        in_specs=whole_vmem(len(operands)),
+        out_specs=whole_vmem(9),
+        scratch_shapes=scratch,
+        compiler_params=pltpu.CompilerParams(collective_id=cid, has_side_effects=True, vmem_limit_bytes=VMEM_LIMIT),
+        name="late",
+    )(*operands)
+
+
 def normalize(row_block):
     centered = row_block - jnp.mean(row_block, axis=-1, keepdims=True)
     inverse = lax.rsqrt(jnp.mean(centered * centered, axis=-1, keepdims=True) + EPSILON)
@@ -461,30 +757,6 @@
         pieces.append(mixture.astype(BF16))
         log_sums.append((highest + jnp.log(totals))[..., 0])
     return (jnp.concatenate(pieces, axis=1), jnp.concatenate(log_sums, axis=2))
-
-
-def attention_backward(queries, keys_all, values_all, grad_attended, log_sums, valid_keys, score_scale, block_rows):
-    grad_keys = jnp.zeros(keys_all.shape, F32)
-    grad_values = jnp.zeros(values_all.shape, F32)
-    grad_pieces = []
-    for offset in range(0, SEQ, block_rows):
-        query_block = queries[:, offset : offset + block_rows]
-        grad_block = grad_attended[:, offset : offset + block_rows]
-        scores = masked_scores(query_block, keys_all, valid_keys, score_scale)
-        softmax_rows = jnp.exp(scores - log_sums[:, :, offset : offset + block_rows, None])
-        grad_probs = jnp.einsum("sqhe,skhe->shqk", grad_block, values_all, preferred_element_type=F32)
-        centre = jnp.sum(softmax_rows * grad_probs, axis=-1, keepdims=True)
-        grad_scores = (softmax_rows * (grad_probs - centre)).astype(BF16)
-        grad_pieces.append(
-            jnp.einsum("shqk,skhe->sqhe", grad_scores, keys_all, preferred_element_type=F32) * score_scale
-        )
-        grad_keys = (
-            grad_keys + jnp.einsum("shqk,sqhe->skhe", grad_scores, query_block, preferred_element_type=F32) * score_scale
-        )
-        grad_values = grad_values + jnp.einsum(
-            "shqk,sqhe->skhe", softmax_rows.astype(BF16), grad_block, preferred_element_type=F32
-        )
-    return (jnp.concatenate(grad_pieces, axis=1), grad_keys, grad_values)
 
 
 def body(
@@ -548,31 +820,46 @@
     grad_inner = gelu_pull(grad_activated)[0].astype(BF16)
     grad_w_inner = dot(second_all, grad_inner, ((0,), (0,))).astype(BF16)
     grad_b_inner = jnp.sum(grad_inner.astype(F32), axis=0)
-    grad_second = tensor_scatter(dot(grad_inner, w_inner, ((1,), (1,))).astype(BF16), 6)
+    second_part = dot(grad_inner, w_inner, ((1,), (1,))).astype(BF16)
+    bias_keys = jnp.broadcast_to(jnp.where(valid_keys[0], 0.0, NEG_LARGE)[:, None], (SEQ, rows_dev))
+    heads_here = w_query.shape[1] // HDIM
+    logs = log_sums.reshape(heads_here, SEQ // rows_dev, rows_dev).transpose(1, 0, 2)
+    (
+        grad_second,
+        grad_hidden,
+        grad_attn_all,
+        grad_queries,
+        grad_keys,
+        grad_values,
+        grad_first,
+        sum_inner,
+        sum_outer,
+    ) = late(
+        dp_count,
+        512,
+        6,
+        second_part,
+        normed_two,
+        inverse_two,
+        cotangent,
+        gain[:, width:],
+        w_out,
+        queries,
+        keys_all,
+        keys_all.T,
+        values_all,
+        logs.reshape(-1, 1, rows_dev),
+        bias_keys,
+        w_query,
+        w_key,
+        w_value,
+        grad_w_inner,
+        grad_w_outer,
+    )
     grad_out_rows = cotangent.astype(F32)
-    grad_hidden = grad_out_rows + norm_back(grad_second * gain[:, width:], normed_two, inverse_two)
-    grad_attn_all = tensor_gather(grad_hidden.astype(BF16), 7)
     grad_w_out = dot(grad_attn_all, attended, ((0,), (0,)))
-    grad_attended = dot(grad_attn_all, w_out, ((1,), (1,))).astype(BF16)
-    grad_q_heads, grad_k_heads, grad_v_heads = attention_backward(
-        split_heads(queries),
-        split_heads(keys_all),
-        split_heads(values_all),
-        split_heads(grad_attended),
-        log_sums,
-        valid_keys,
-        score_scale,
-        block_rows,
-    )
-    grad_queries = grad_q_heads.reshape(queries.shape).astype(BF16)
-    grad_keys = grad_k_heads.reshape(queries.shape).astype(BF16)
-    grad_values = grad_v_heads.reshape(queries.shape).astype(BF16)
     grad_b_query = jnp.sum(grad_queries.astype(F32), axis=0)
     grad_b_value = jnp.sum(grad_values.astype(F32), axis=0)
-    total_rows = dot(grad_queries, w_query, ((1,), (1,)))
-    total_rows = total_rows + dot(grad_keys, w_key, ((1,), (1,)))
-    total_rows = total_rows + dot(grad_values, w_value, ((1,), (1,)))
-    grad_first = tensor_scatter(total_rows.astype(BF16), 8)
     grad_w_attn = jnp.concatenate(
         [
             dot(first_all, grad_queries, ((0,), (0,))).astype(BF16),
@@ -596,9 +883,7 @@
     bias = jnp.concatenate(
         [grad_b_inner, grad_b_query, grad_b_value, jnp.zeros((2048 - 1024 - 512,), F32)]
     ).reshape(16, 128)
-    sum_inner, sum_outer, sum_attn, small = dp_sum(
-        dp_count, [grad_w_inner, grad_w_outer, grad_w_attn], [512, 512, 512], vec, bias, pick, 9
-    )
+    sum_attn, small = dp_sum(dp_count, [grad_w_attn], [256], vec, bias, pick, 9)
     small = small.astype(F32)
     tables = small[: 32 * sections].reshape(sections, 2, 2 * width)
     shared = small[32 * sections : 32 * sections + 16].reshape(2, width)

time: 460 us -> 383 us (0.83)
  matrix products: 96 us -> 59 us
  Pallas kernels: 297 us -> 266 us
  other arithmetic: 46.7 us -> 33.8 us
    pallas_call x0 -> x1, Pallas kernels: none -> 111 us  [late(): pl.pallas_call(functools.partial(late_kernel, count, width), out_shape=[s...]
    pallas_call x1, Pallas kernels: 153 us -> 63.7 us  [dp_sum(): pl.pallas_call(functools.partial(dp_sum_kernel, count, tuple(widths)), ou...]
    pallas_call x4 -> x2, Pallas kernels: 72.9 us -> 36.7 us  [tensor_scatter(): pl.pallas_call(scatter_kernel, out_shape=jax.ShapeDtypeStruct((rows, widt...]
    dot_general x8 -> x0, matrix products: 30.8 us -> none  [the longest x2 19.3 us: attention_backward(): jnp.einsum('sqhe,skhe->shqk', grad_block, values_all, preferred_element_t...]
    pallas_call x4 -> x3, Pallas kernels: 71.6 us -> 54 us  [tensor_gather(): pl.pallas_call(gather_kernel, out_shape=jax.ShapeDtypeStruct((rows * 4, w...]
    convert_element_type x2 -> x0, other arithmetic: 9.88 us -> none  [the longest x1 9.01 us: attention_backward(): grad_scores = (softmax_rows * (grad_probs - centre)).astype(BF16)]
    dot_general x18 -> x14, matrix products: 56.5 us -> 47.1 us  [dot(): return lax.dot_general(a, b, (dims, ((), ())), preferred_element_type=F32)]
where the time goes in v2:
time: 383 us; the launch traced here: 376 us
  Pallas kernels  266 us (69%)
  matrix products  59 us (15%)
  other arithmetic  33.8 us (9%)
  local copies, waits for them, and re-layouts  14.7 us (4%)
    pallas_call x1, Pallas kernels, late(): pl.pallas_call(functools.partial(late_kernel, count, width), out_shape=[s...  111 us
    pallas_call x1, Pallas kernels, dp_sum(): pl.pallas_call(functools.partial(dp_sum_kernel, count, tuple(widths)), ou...  63.7 us
    pallas_call x3, Pallas kernels, tensor_gather(): pl.pallas_call(gather_kernel, out_shape=jax.ShapeDtypeStruct((rows * 4, w...  54 us
    dot_general x14, matrix products, dot(): return lax.dot_general(a, b, (dims, ((), ())), preferred_element_type=F32)  47.1 us
    pallas_call x2, Pallas kernels, tensor_scatter(): pl.pallas_call(scatter_kernel, out_shape=jax.ShapeDtypeStruct((rows, widt...  36.7 us

profile of v2, /device:TPU:0, one launch (start us, length us, event | category | flops | bytes accessed | tf_op | source)
XLA Modules:
  0.0 376.2 jit_solution(14366400566809971092)
XLA Ops:
  2.1 1.2 convert_reduce_fusion.1
  3.3 1.3 fusion.31
  5.3 1.1 convert_reduce_fusion.4
  7.2 0.9 constant_dynamic-slice_fusion
  8.1 2.1 fusion.25.x_ref
  10.2 1.2 broadcast_in_dim.34.refs_11_
  11.4 19.1 %tensor_gather_1.1 = bf16[1024,1024]{1,0:T(8,128)(2,1)} custom-call(bf16[256,1024]{1,0:T(8,128)(2,1)} %fusion.25.x_ref), custom_call_target="tpu_custom_call" | custom-call | tf_op jit(solution)/shard_map/tensor_gather_1/pallas_call | solution.py:79
  30.5 2.3 convolution_convert_fusion.9
  33.0 2.5 fusion.13.refs_6_
  35.5 1.5 fusion.12.refs_9_
  37.0 2.0 copy.48
  39.1 1.0 copy.50
  40.1 1.0 copy.52.refs_7_
  41.1 17.7 %tensor_gather_4.1 = bf16[1024,1024]{1,0:T(8,128)(2,1)} custom-call(bf16[256,1024]{1,0:T(8,128)(2,1)} %refs_3_.1), custom_call_target="tpu_custom_call" | custom-call | tf_op jit(solution)/shard_map/tensor_gather_4/pallas_call | solution.py:79
  58.8 2.4 fusion
  61.2 3.4 fusion.2
  64.6 3.0 fusion.22
  67.6 2.0 fusion.3
  69.6 3.1 fusion.23
  73.4 1.0 pad_maximum_fusion.1
  74.5 0.8 copy-done.13
  75.3 2.1 convolution_convert_fusion.4.p_ref
  77.3 18.4 %tensor_scatter_2.1 = f32[256,1024]{1,0:T(8,128)} custom-call(bf16[1024,1024]{1,0:T(8,128)(2,1)} %convolution_convert_fusion.4.p_ref), custom_call_target="tpu_custom_call" | custom-call | tf_op jit(solution)/shard_map/tensor_scatter_2/pallas_call | solution.py:131
  95.7 1.4 fusion.40
  97.2 1.5 multiply_reduce_fusion.1
  98.7 0.8 copy.51.refs_2_
  99.5 2.7 add_convert_fusion.2
  102.2 17.2 %tensor_gather_3.1 = bf16[1024,1024]{1,0:T(8,128)(2,1)} custom-call(bf16[256,1024]{1,0:T(8,128)(2,1)} %get-tuple-element.80.x_ref), custom_call_target="tpu_custom_call" | custom-call | tf_op jit(solution)/shard_map/tensor_gather_3/pallas_call | solution.py:79
  119.4 4.7 %fusion.46 = f32[1024,1024]{1,0:T(8,128)S(1)} fusion(bf16[1024,1024]{1,0:T(8,128)(2,1)} %tensor_gather_3.1, bf16[1024,1024]{1,0:T(8,128)(2,1)} %param.29), kind=kOutput, calls=%fused_computation.122 | convolution fusion | flops 2147483648 | bytes 8388608 | tf_op jit(solution)/shard_map/dot_general | solution.py:739
  124.1 12.2 %convert_reduce_fusion = (f32[1024]{0:T(1024)S(1)}, bf16[1024,1024]{1,0:T(8,128)(2,1)S(1)}, f32[1024,1024]{1,0:T(8,128)S(1)}) fusion(f32[1024,1024]{1,0:T(8,128)S(1)} %fusion.46, f32[1024]{0:T(1024)S(1)} %copy-done.26, bf16[1024,1024]{1,0:T(8,128)(2,1)S(1)} %copy-done.9, bf16[1024,1024]{1,0:T(8,128)(2,1)S(1)} %copy-done), kind=kOutput, calls=%fused_computation.12 | convolution fusion | flops 2226125824 | bytes 14688256 | tf_op jit(solution)/shard_map/dot_general | solution.py:739
  136.3 3.8 %convolution_convert_fusion.1.refs_15_ = bf16[1024,1024]{1,0:T(8,128)(2,1)} fusion(bf16[1024,1024]{1,0:T(8,128)(2,1)S(1)} %copy-done.10, bf16[1024,1024]{1,0:T(8,128)(2,1)S(1)} %get-tuple-element.76), kind=kOutput, calls=%fused_computation.32 | convolution fusion | flops 2148532224 | bytes 6291456 | tf_op jit(solution)/shard_map/dot_general | solution.py:739
  140.1 1.1 multiply_convert_fusion
  141.3 3.8 %convolution_convert_fusion.refs_16_ = bf16[1024,1024]{1,0:T(8,128)(2,1)} fusion(bf16[1024,1024]{1,0:T(8,128)(2,1)S(1)} %multiply_convert_fusion, bf16[1024,1024]{1,0:T(8,128)(2,1)S(1)} %copy-done.9), kind=kOutput, calls=%fused_computation.31 | convolution fusion | flops 2148532224 | bytes 6291456 | tf_op jit(solution)/shard_map/dot_general | solution.py:739
  145.1 3.7 convolution_convert_fusion.3.p_ref
  148.8 18.3 %tensor_scatter_5.1 = f32[256,1024]{1,0:T(8,128)} custom-call(bf16[1024,1024]{1,0:T(8,128)(2,1)} %convolution_convert_fusion.3.p_ref), custom_call_target="tpu_custom_call" | custom-call | tf_op jit(solution)/shard_map/tensor_scatter_5/pallas_call | solution.py:131
  167.1 5.9 %convolution_convert_fusion.2.refs_0_ = bf16[1024,1024]{1,0:T(8,128)(2,1)} fusion(bf16[1024,1024]{1,0:T(8,128)(2,1)} %copy-done.31, bf16[1024,1024]{1,0:T(8,128)(2,1)} %param.29), kind=kOutput, calls=%fused_computation.33 | convolution fusion | flops 2148532224 | bytes 6291456 | tf_op jit(solution)/shard_map/dot_general | solution.py:739
  173.0 111.2 %late.1 = (f32[256,1024]{1,0:T(8,128)}, f32[256,1024]{1,0:T(8,128)}, bf16[1024,1024]{1,0:T(8,128)(2,1)}, bf16[1024,256]{1,0:T(8,128)(2,1)}, bf16[1024,256]{1,0:T...) custom-call(bf16[1024,1024]{1,0:T(8,128)(2,1)} %convolution_convert_, ...), custom_call_target="tpu_custom_call" | custom-call | tf_op jit(solution)/shard_map/late/pallas_call | solution.py:695
  284.2 1.9 fusion.41
  286.1 2.4 convolution_convert_fusion.5
  291.3 1.6 pad_maximum_fusion.refs_0_
  294.2 1.6 fusion.44
  296.5 63.7 %dp_sum.1 = (bf16[1024,1024]{1,0:T(8,128)(2,1)}, bf16[256,128]{1,0:T(8,128)(2,1)}) custom-call(bf16[1024,1024]{1,0:T(8,128)(2,1)} %pad_maximum_fusion.refs_0_, f32[48,128]{1,0:T(8,128)} %copy-done.25, f32[16,128]{1,0:T(8,128)} %maximum_bitcast_fusion.refs_2_, f32[7,128]{1,0:T(8,128)} %broadcast_in_dim.36.refs_3_), custom_call_target="tpu_custom_call" | custom-call | tf_op jit(solution)/shard_map/dp_sum/pallas_call | solution.py:408
  360.2 0.8 slice.97
  361.8 0.8 convert_element_type.157
  364.5 3.3 convert_bitcast_fusion
  367.8 1.3 copy.59
  369.1 4.2 %convert_element_type.163 = f32[1024,1024]{1,0:T(8,128)} convert(bf16[1024,1024]{1,0:T(8,128)(2,1)} %get-tuple-element.35) | non-fusion elementwise | flops 1048576 | bytes 6291456 | tf_op jit(solution)/shard_map/convert_element_type | solution.py:905
  373.3 2.5 convert_element_type.164
  (96 shorter events, 9.5 us)
Async XLA Ops:
  0.6 123.5 %copy-start = (bf16[1024,1024]{1,0:T(8,128)(2,1)S(1)}, bf16[1024,1024]{1,0:T(8,128)(2,1)}, u32[]{:S(2)}) copy-start(bf16[1024,1024]{1,0:T(8,128)(2,1)} %param.31) | copy-start | bytes 6291460
  0.7 29.9 %copy-start.18 = (bf16[1024,256]{1,0:T(8,128)(2,1)S(1)}, bf16[1024,256]{1,0:T(8,128)(2,1)}, u32[]{:S(2)}) copy-start(bf16[1024,256]{1,0:T(8,128)(2,1)} %refs_13_.1) | copy-start | bytes 1572868
  6.5 26.5 %copy-start.19 = (bf16[1024,256]{1,0:T(8,128)(2,1)S(1)}, bf16[1024,256]{1,0:T(8,128)(2,1)}, u32[]{:S(2)}) copy-start(bf16[1024,256]{1,0:T(8,128)(2,1)} %refs_12_.1) | copy-start | bytes 1572868
  6.5 26.5 %copy-start.29 = (f32[256]{0:T(256)S(1)}, f32[256]{0:T(256)}, u32[]{:S(2)}) copy-start(f32[256]{0:T(256)} %param.23) | copy-start | bytes 3076
  8.1 91.4 %copy-start.24 = (f32[1,1024]{1,0:T(1,128)}, f32[1,1024]{1,0:T(1,128)S(1)}, u32[]{:S(2)}) copy-start(f32[1,1024]{1,0:T(1,128)S(1)} %get-tuple-element.97.refs_4_) | copy-start | bytes 12292
  32.9 28.3 %copy-start.3 = (bf16[1024,256]{0,1:T(8,128)(2,1)}, bf16[1024,256]{0,1:T(8,128)(2,1)S(1)}, u32[]{:S(2)}) copy-start(bf16[1024,256]{0,1:T(8,128)(2,1)S(1)} %convolution_convert_fusion.9) | copy-start | bytes 1572868
  32.9 2.6 copy-start.7
  32.9 2.6 copy-start.17
  32.9 2.6 copy-start.30
  35.5 4.6 %copy-start.11 = (bf16[1024,256]{1,0:T(8,128)(2,1)}, bf16[1024,256]{1,0:T(8,128)(2,1)S(1)}, u32[]{:S(2)}) copy-start(bf16[1024,256]{1,0:T(8,128)(2,1)S(1)} %fusion.13.refs_6_) | copy-start | bytes 1572868
  58.7 2.4 copy-start.15
  61.2 3.4 copy-start.22
  69.6 5.6 %copy-start.12 = (bf16[256,1024]{1,0:T(8,128)(2,1)S(1)}, bf16[256,1024]{1,0:T(8,128)(2,1)}, u32[]{:S(2)}) copy-start(bf16[256,1024]{1,0:T(8,128)(2,1)} %refs_5_.1) | copy-start | bytes 1572868
  72.8 22.9 %copy-start.1 = (bf16[256,1024]{1,0:T(8,128)(2,1)S(1)}, bf16[256,1024]{1,0:T(8,128)(2,1)}, u32[]{:S(2)}) copy-start(bf16[256,1024]{1,0:T(8,128)(2,1)} %param.18) | copy-start | bytes 1572868
  72.8 23.0 %copy-start.23 = (f32[1024]{0:T(1024)S(1)}, f32[1024]{0:T(1024)}, u32[]{:S(2)}) copy-start(f32[1024]{0:T(1024)} %param.28) | copy-start | bytes 12292
  74.4 0.8 copy-start.13
  119.4 4.7 %copy-start.9 = (bf16[1024,1024]{1,0:T(8,128)(2,1)S(1)}, bf16[1024,1024]{1,0:T(8,128)(2,1)}, u32[]{:S(2)}) copy-start(bf16[1024,1024]{1,0:T(8,128)(2,1)} %tensor_gather_4.1) | copy-start | bytes 6291460
  119.4 4.7 %copy-start.26 = (f32[1024]{0:T(1024)S(1)}, f32[1024]{0:T(1024)}, u32[]{:S(2)}) copy-start(f32[1024]{0:T(1024)} %param.30) | copy-start | bytes 12292
  124.1 12.2 %copy-start.10 = (bf16[1024,1024]{1,0:T(8,128)(2,1)S(1)}, bf16[1024,1024]{1,0:T(8,128)(2,1)}, u32[]{:S(2)}) copy-start(bf16[1024,1024]{1,0:T(8,128)(2,1)} %tensor_gather_3.1) | copy-start | bytes 6291460
  136.3 3.8 %copy-start.31 = (bf16[1024,1024]{1,0:T(8,128)(2,1)}, bf16[1024,1024]{1,0:T(8,128)(2,1)S(1)}, u32[]{:S(2)}) copy-start(bf16[1024,1024]{1,0:T(8,128)(2,1)S(1)} %get-tuple-element.76) | copy-start | bytes 6291460
  173.0 113.1 %copy-start.14 = (bf16[1,1024,4,64]{1,3,2,0:T(8,128)(2,1)S(1)}, bf16[1,1024,4,64]{1,3,2,0:T(8,128)(2,1)}, u32[]{:S(2)}) copy-start(bf16[1,1024,4,64]{1,3,2,0:T(8,128)(2,1)} %copy-done.13) | copy-start | bytes 1572868
  284.2 4.3 %copy-start.21 = (bf16[1024,256]{1,0:T(8,128)(2,1)S(1)}, bf16[1024,256]{1,0:T(8,128)(2,1)}, u32[]{:S(2)}) copy-start(bf16[1024,256]{1,0:T(8,128)(2,1)} %get-tuple-element.28) | copy-start | bytes 1572868
  284.2 4.4 %copy-start.8 = (bf16[1024,1024]{1,0:T(8,128)(2,1)S(1)}, bf16[1024,1024]{1,0:T(8,128)(2,1)}, u32[]{:S(2)}) copy-start(bf16[1024,1024]{1,0:T(8,128)(2,1)} %tensor_gather_1.1) | copy-start | bytes 6291460
  288.4 1.0 copy-start.20
  289.5 1.0 copy-start.28
  290.5 3.0 copy-start.5
  291.3 2.8 copy-start.2
  291.3 2.8 copy-start.4
  291.3 2.8 copy-start.16
  291.3 2.8 copy-start.27
  295.8 0.6 copy-start.25
  369.1 4.2 %copy-start.6 = (bf16[1024,1024]{1,0:T(8,128)(2,1)S(1)}, bf16[1024,1024]{1,0:T(8,128)(2,1)}, u32[]{:S(2)}) copy-start(bf16[1024,1024]{1,0:T(8,128)(2,1)} %get-tuple-element.36) | copy-start | bytes 6291460

commit v3 on v2

--- a/solution.py
+++ b/solution.py
@@ -183,7 +183,7 @@
     part = rows // 2
     for size in sizes[1:]:
         part //= size
-        shapes += [pltpu.VMEM((size, part, width), BF16)] * 2
+        shapes += [pltpu.VMEM((size - 1, part, width), BF16)] * 2
     return shapes
 
 
@@ -237,26 +237,27 @@
                 at_end = (z == 0) if way == 0 else (z == n - 1)
                 slot = (right_slot if way == 0 else left_slot) + jnp.clip(o, 0, n - 1)
                 o = jnp.clip(o, 0, n - 1)
+                at = jnp.clip(o - 1 + way, 0, n - 2)
                 there = line.right if way == 0 else line.left
-                copy = remote(own.at[piece(o)], buffer.at[o], send.at[slot], recv.at[slot], there)
-                onward = remote(buffer.at[o], buffer.at[o], send.at[slot], recv.at[slot], there)
+                copy = remote(own.at[piece(o)], buffer.at[at], send.at[slot], recv.at[slot], there)
+                onward = remote(buffer.at[at], buffer.at[at], send.at[slot], recv.at[slot], there)
                 go(copy, inside & at_end)
 
-                def pass_on(buffer=buffer, o=o, onward=onward, piece=piece):
+                def pass_on(buffer=buffer, o=o, at=at, onward=onward, piece=piece):
                     onward.wait_recv()
-                    buffer[o] = (buffer[o].astype(F32) + own[piece(o), :].astype(F32)).astype(BF16)
+                    buffer[at] = (buffer[at].astype(F32) + own[piece(o), :].astype(F32)).astype(BF16)
                     onward.start()
 
                 when(inside & jnp.logical_not(at_end), pass_on)
                 started.append((onward, inside & jnp.logical_not(at_end)))
             yield
 
-        def take(buffer, slot, line=line, piece=piece, z=z):
-            remote(buffer.at[z], buffer.at[z], send.at[slot + z], recv.at[slot + z], line.right).wait_recv()
-            own[piece(z), :] = (own[piece(z), :].astype(F32) + buffer[z].astype(F32)).astype(BF16)
-
-        when(z > 0, functools.partial(take, to_right, right_slot))
-        when(z < n - 1, functools.partial(take, to_left, left_slot))
+        def take(buffer, slot, at, line=line, piece=piece, z=z):
+            remote(buffer.at[at], buffer.at[at], send.at[slot + z], recv.at[slot + z], line.right).wait_recv()
+            own[piece(z), :] = (own[piece(z), :].astype(F32) + buffer[at].astype(F32)).astype(BF16)
+
+        when(z > 0, functools.partial(take, to_right, right_slot, jnp.maximum(z - 1, 0)))
+        when(z < n - 1, functools.partial(take, to_left, left_slot, jnp.minimum(z, n - 2)))
         base = bases + z * part
         size_now = part
     final = pl.ds(pl.multiple_of(mine + base, size_now), size_now)
@@ -309,120 +310,16 @@
             when(condition, lambda copy=copy: copy.wait_send())
 
 
-def run_skewed(makers):
-    makers = list(makers)
-    running = []
-    while makers or running:
-        if makers:
-            running.append(makers.pop(0)())
-        still = []
-        for generator in running:
-            try:
-                next(generator)
-                still.append(generator)
-            except StopIteration:
-                pass
-        running = still
-
-
-def dp_sum_kernel(count, widths, *refs):
-    arrays = len(widths)
-    ins, rest = refs[:arrays], refs[arrays:]
-    vec_ref, bias_ref, pick_ref = rest[:3]
-    outs, rest = rest[3 : 3 + arrays], rest[3 + arrays :]
-    small_out, rest = rest[0], rest[1:]
-    small_in, vec_got, vec_send, vec_recv = rest[:4]
-    rest = rest[4:]
-    dp, me, sib, across, diag = places()
-    lines = lines_of(count, dp, me)
-    others = [lines[0].pair]
-    near = [(dp, sib), (dp, across), (dp, diag)]
-    barrier = pltpu.get_barrier_semaphore()
-    for partner in near + others:
-        pl.semaphore_signal(barrier, inc=1, device_id=partner, device_id_type=MESH)
-    waits = len(near) + len(others)
-    for line in lines[1:]:
-        has_right = line.place < line.size - 1
-        has_left = line.place > 0
-        for partner, has in ((line.right, has_right), (line.left, has_left)):
-            pl.when(has)(
-                lambda partner=partner: pl.semaphore_signal(
-                    barrier, inc=1, device_id=partner, device_id_type=MESH
-                )
-            )
-        waits = waits + has_right.astype(jnp.int32) + has_left.astype(jnp.int32)
-    pl.semaphore_wait(barrier, waits)
-    vec_copies = []
-    for i, device in enumerate(near):
-        vec_copies.append(remote(vec_ref, vec_got.at[i], vec_send.at[i], vec_recv.at[i], device))
-        vec_copies[-1].start()
-
-    per = 2 + 2 * (len(lines) - 1)
-    makers = []
-    for array in range(arrays):
-        wide = ins[array].shape[1]
-        for start in range(0, wide, widths[array]):
-            scratch, rest = rest[:per], rest[per:]
-            send, recv = rest[:2]
-            rest = rest[2:]
-            makers.append(
-                functools.partial(
-                    sum_chunk, lines, ins[array], outs[array], pl.ds(start, widths[array]), scratch, send, recv
-                )
-            )
-
-    def small():
-        for copy in vec_copies:
-            copy.wait_recv()
-        total = vec_ref[...] + vec_got[0] + vec_got[1] + vec_got[2]
-        sections = pick_ref.shape[0]
-        for s in range(sections):
-            small_in[pl.ds(32 * s, 32), :] = (total[0:32] * pick_ref[s : s + 1, :]).astype(BF16)
-        small_in[pl.ds(32 * sections, 16), :] = total[32:48].astype(BF16)
-        small_in[pl.ds(32 * sections + 16, 16), :] = bias_ref[...].astype(BF16)
-        done = 32 * sections + 32
-        if done < small_in.shape[0]:
-            small_in[pl.ds(done, small_in.shape[0] - done), :] = jnp.zeros((small_in.shape[0] - done, 128), BF16)
-        yield from sum_chunk(lines, small_in, small_out, slice(None), rest[:per], rest[per], rest[per + 1])
-
-    run_skewed(makers + [small])
-    for copy in vec_copies:
-        copy.wait_send()
-
-
-def dp_sum(count, grads, widths, vec, bias, pick, cid):
-    small_rows = max(16 * count, -(-(32 * pick.shape[0] + 32) // (16 * count)) * 16 * count)
-    sems = chunk_sems(count)
-    scratch = [
-        pltpu.VMEM((small_rows, 128), BF16),
-        pltpu.VMEM((3,) + vec.shape, F32),
-        pltpu.SemaphoreType.DMA((3,)),
-        pltpu.SemaphoreType.DMA((3,)),
-    ]
-    for grad, width in zip(grads, widths):
-        for _ in range(0, grad.shape[1], width):
-            scratch += chunk_scratch(count, grad.shape[0], width)
-            scratch += [pltpu.SemaphoreType.DMA((sems,))] * 2
-    scratch += chunk_scratch(count, small_rows, 128)
-    scratch += [pltpu.SemaphoreType.DMA((sems,))] * 2
-    return pl.pallas_call(
-        functools.partial(dp_sum_kernel, count, tuple(widths)),
-        out_shape=[jax.ShapeDtypeStruct(g.shape, BF16) for g in grads]
-        + [jax.ShapeDtypeStruct((small_rows, 128), BF16)],
-        in_specs=whole_vmem(len(grads) + 3),
-        out_specs=whole_vmem(len(grads) + 1),
-        scratch_shapes=scratch,
-        compiler_params=pltpu.CompilerParams(collective_id=cid, has_side_effects=True, vmem_limit_bytes=VMEM_LIMIT),
-        name="dp_sum",
-    )(*grads, vec, bias, pick)
-
-
 class Turns:
     def __init__(self, generators):
         self.waiting = list(generators)
         self.running = []
         for generator in self.waiting:
             next(generator)
+
+    def add(self, generator):
+        next(generator)
+        self.waiting.append(generator)
 
     def turn(self):
         if self.waiting:
@@ -504,24 +401,36 @@
             copy.wait_send()
 
 
+def norm_parts(block):
+    centered = block - jnp.mean(block, axis=-1, keepdims=True)
+    inverse = lax.rsqrt(jnp.mean(centered * centered, axis=-1, keepdims=True) + EPSILON)
+    return centered * inverse, inverse
+
+
+def column_sums(block):
+    return jnp.sum(block, axis=0, keepdims=True)
+
+
 def late_kernel(count, width, *refs):
-    p_ref, normed_ref, inverse_ref, cot_ref, gain_ref, w_out_ref = refs[:6]
-    q_ref, k_ref, kt_ref, v_ref, log_ref, bias_ref = refs[6:12]
-    wq_ref, wk_ref, wv_ref, gi_ref, go_ref = refs[12:17]
-    gsec_ref, ghid_ref, gattn_ref, dq_ref, dk_ref, dv_ref, gfirst_ref, si_ref, so_ref = refs[17:26]
-    rest = refs[26:]
+    p_ref, po_ref, hidden_ref, frames_ref, cot_ref, gain_ref, b_outer_ref = refs[:7]
+    w_out_ref, q_ref, k_ref, kt_ref, v_ref, log_ref, bias_ref = refs[7:14]
+    wq_ref, wk_ref, wv_ref, first_ref, att_ref, gi_ref, go_ref, gb_ref, pick_ref = refs[14:23]
+    out_ref, fgrad_ref, si_ref, so_ref, sa_ref, small_ref = refs[23:29]
+    rest = refs[29:]
     from_one, chip_one, landed_one, send_one, recv_one = rest[:5]
     from_two, chip_two, landed_two, send_two, recv_two = rest[5:10]
-    total_ref, gsend, grecv = rest[10:13]
-    do_cat, q_cat, p_scr, ds_scr, dk_acc, dv_acc, dqt_ref = rest[13:20]
-    rest = rest[20:]
+    from_out, chip_out, landed_out, send_out, recv_out = rest[10:15]
+    gsend, grecv, vec_got, vec_send, vec_recv = rest[15:20]
+    gattn_ref, gsec_ref, ghid_ref, dqkv_ref, vec_ref, small_in = rest[20:26]
+    do_cat, q_cat, p_scr, ds_scr, dk_acc, dv_acc, dqt_ref = rest[26:33]
+    rest = rest[33:]
     spot = places()
     dp, me, sib, across, diag = spot
     lines = lines_of(count, dp, me)
     barrier = pltpu.get_barrier_semaphore()
-    for partner in [(dp, sib), (dp, across), lines[0].pair]:
+    for partner in [(dp, sib), (dp, across), (dp, diag), lines[0].pair]:
         pl.semaphore_signal(barrier, inc=1, device_id=partner, device_id_type=MESH)
-    waits = 3
+    waits = 4
     for line in lines[1:]:
         has_right = line.place < line.size - 1
         has_left = line.place > 0
@@ -534,19 +443,26 @@
         waits = waits + has_right.astype(jnp.int32) + has_left.astype(jnp.int32)
     pl.semaphore_wait(barrier, waits)
 
-    rows = normed_ref.shape[0]
+    rows, model = hidden_ref.shape
+    local = q_ref.shape[1]
     one = Scatter(spot, p_ref, from_one, chip_one, landed_one, send_one, recv_one)
+    outer = Scatter(spot, po_ref, from_out, chip_out, landed_out, send_out, recv_out)
     one.start_first()
     one.start_last()
+    outer.start_first()
+    outer.start_last()
     per = 2 + 2 * (len(lines) - 1)
-    chunks = []
-    for x_ref, o_ref in ((gi_ref, si_ref), (go_ref, so_ref)):
-        for start in range(0, x_ref.shape[1], width):
-            chunks.append(
-                sum_chunk(lines, x_ref, o_ref, pl.ds(start, width), rest[:per], rest[per], rest[per + 1])
-            )
+
+    def chunks_of(x_ref, o_ref):
+        nonlocal rest
+        made = []
+        wide = min(width, x_ref.shape[1])
+        for start in range(0, x_ref.shape[1], wide):
+            made.append(sum_chunk(lines, x_ref, o_ref, pl.ds(start, wide), rest[:per], rest[per], rest[per + 1]))
             rest = rest[per + 2 :]
-    turns = Turns(chunks)
+        return made
+
+    turns = Turns(chunks_of(gi_ref, si_ref) + chunks_of(go_ref, so_ref))
     one.cross()
 
     dk_acc[...] = jnp.zeros_like(dk_acc)
@@ -557,18 +473,19 @@
     def block_part(owner, i):
         return gattn_ref.at[pl.ds(pl.multiple_of(owner * rows + i * part, part), part)]
 
+    def back(values, grad_hat):
+        normed, inverse = norm_parts(values)
+        return inverse * (
+            grad_hat
+            - jnp.mean(grad_hat, axis=-1, keepdims=True)
+            - normed * jnp.mean(grad_hat * normed, axis=-1, keepdims=True)
+        )
+
     for i in range(PARTS):
         here = pl.ds(i * part, part)
         grad_second = one.result(i)
         gsec_ref[here, :] = grad_second
-        normed = normed_ref[here, :]
-        grad_hat = grad_second * gain_ref[...]
-        back = inverse_ref[here, :] * (
-            grad_hat
-            - jnp.mean(grad_hat, axis=-1, keepdims=True)
-            - normed * jnp.mean(grad_hat * normed, axis=-1, keepdims=True)
-        )
-        grad_hidden = cot_ref[here, :].astype(F32) + back
+        grad_hidden = cot_ref[here, :].astype(F32) + back(hidden_ref[here, :], grad_second * gain_ref[1:2, :])
         ghid_ref[here, :] = grad_hidden
         gattn_ref[pl.ds(pl.multiple_of(me * rows + i * part, part), part), :] = grad_hidden.astype(BF16)
         ref = block_part(me, i)
@@ -577,10 +494,11 @@
         to_sib.append(remote(ref, ref, gsend.at[PARTS + i], grecv.at[PARTS + i], (dp, sib)))
         to_sib[-1].start()
     turns.turn()
-
-    heads = q_ref.shape[1] // HDIM
+    outer.cross()
+
+    heads = local // HDIM
     scale = HDIM ** (-0.5)
-    lanes = lax.broadcasted_iota(jnp.int32, (rows, q_ref.shape[1]), 1) // HDIM
+    lanes = lax.broadcasted_iota(jnp.int32, (rows, local), 1) // HDIM
 
     def attend(owner):
         block = pl.ds(pl.multiple_of(owner * rows, rows), rows)
@@ -629,18 +547,19 @@
     attend(diag)
     turns.turn()
 
-    dk_ref[...] = (dk_acc[...] * scale).astype(BF16)
-    dv_ref[...] = dv_acc[...].astype(BF16)
+    dqkv_ref[:, pl.ds(local, local)] = (dk_acc[...] * scale).astype(BF16)
+    dqkv_ref[:, pl.ds(2 * local, local)] = dv_acc[...].astype(BF16)
+    total_ref = p_scr
     two = Scatter(spot, total_ref, from_two, chip_two, landed_two, send_two, recv_two)
 
     def total(owner):
         block = pl.ds(pl.multiple_of(owner * rows, rows), rows)
         grad_query = (dqt_ref[owner].T * scale).astype(BF16)
-        dq_ref[block, :] = grad_query
+        dqkv_ref[block, pl.ds(0, local)] = grad_query
         total_ref[block, :] = (
             dot(grad_query, wq_ref[...], ((1,), (1,)))
-            + dot(dk_ref[block, :], wk_ref[...], ((1,), (1,)))
-            + dot(dv_ref[block, :], wv_ref[...], ((1,), (1,)))
+            + dot(dqkv_ref[block, pl.ds(local, local)], wk_ref[...], ((1,), (1,)))
+            + dot(dqkv_ref[block, pl.ds(2 * local, local)], wv_ref[...], ((1,), (1,)))
         ).astype(BF16)
 
     total(diag)
@@ -651,21 +570,94 @@
     two.start_last()
     total(me)
     turns.turn()
+
+    grads_ref = ds_scr
+
+    @pl.loop(0, model // rows)
+    def _(i):
+        at = pl.ds(pl.multiple_of(i * rows, rows), rows)
+        grads_ref[at, pl.ds(0, 3 * local)] = dot(first_ref[:, at], dqkv_ref[...], ((0,), (0,))).astype(BF16)
+        grads_ref[at, pl.ds(3 * local, local)] = dot(gattn_ref[:, at], att_ref[...], ((0,), (0,))).astype(BF16)
+
+    for chunk in chunks_of(grads_ref, sa_ref):
+        turns.add(chunk)
+    turns.turn()
+
+    def put(row, sums):
+        for j in range(sums.shape[1] // 128):
+            vec_ref[pl.ds(row + j, 1), :] = sums[:, j * 128 : (j + 1) * 128]
+
+    vec_ref[...] = jnp.zeros_like(vec_ref)
+    units = gb_ref.shape[0]
+    per_row = model // 128
+    sums = [jnp.zeros((1, model), F32) for _ in range(6)]
     for i in range(PARTS):
-        gfirst_ref[pl.ds(i * part, part), :] = two.result(i)
+        here = pl.ds(i * part, part)
+        grad_first = two.result(i)
+        values = frames_ref[here, :].astype(F32)
+        normed_one, _ = norm_parts(values)
+        normed_two, _ = norm_parts(hidden_ref[here, :])
+        grad_hidden = ghid_ref[here, :]
+        grad_second = gsec_ref[here, :]
+        fgrad_ref[here, :] = grad_hidden + back(values, grad_first * gain_ref[0:1, :])
+        for k, block in enumerate(
+            (
+                grad_first * normed_one,
+                grad_second * normed_two,
+                grad_first,
+                grad_second,
+                grad_hidden,
+                cot_ref[here, :].astype(F32),
+            )
+        ):
+            sums[k] = sums[k] + column_sums(block)
+    for k in range(6):
+        put(k * per_row, sums[k])
+    base = 6 * per_row
+    shared = base
+    near = [(dp, sib), (dp, across), (dp, diag)]
+    vec_copies = [
+        remote(vec_ref.at[pl.ds(0, shared)], vec_got.at[i], vec_send.at[i], vec_recv.at[i], device)
+        for i, device in enumerate(near)
+    ]
+    for copy in vec_copies:
+        copy.start()
+    turns.turn()
+    vec_ref[pl.ds(base, units), :] = gb_ref[...]
+    put(base + units, column_sums(dqkv_ref[:, pl.ds(0, local)].astype(F32)))
+    put(base + units + local // 128, column_sums(dqkv_ref[:, pl.ds(2 * local, local)].astype(F32)))
+    for i in range(PARTS):
+        here = pl.ds(i * part, part)
+        out_ref[here, :] = (hidden_ref[here, :] + outer.result(i) + b_outer_ref[...]).astype(BF16)
+    for copy in vec_copies:
+        copy.wait_recv()
+    every = vec_ref[pl.ds(0, shared), :] + vec_got[0] + vec_got[1] + vec_got[2]
+    sections = pick_ref.shape[0]
+    small_in[...] = jnp.zeros_like(small_in)
+    table = 4 * per_row
+    for k in range(sections):
+        small_in[pl.ds(table * k, table), :] = (every[0:table] * pick_ref[k : k + 1, :]).astype(BF16)
+    done = table * sections
+    small_in[pl.ds(done, shared - table), :] = every[table:shared].astype(BF16)
+    done += shared - table
+    small_in[pl.ds(done, 16), :] = vec_ref[pl.ds(base, 16), :].astype(BF16)
+    for chunk in chunks_of(small_in, small_ref):
+        turns.add(chunk)
     turns.drain()
     one.finish()
     two.finish()
-    for copy in to_across + to_sib + passed:
+    outer.finish()
+    for copy in to_across + to_sib + passed + vec_copies:
         copy.wait_send()
 
 
 def late(count, width, cid, *operands):
-    normed, q, gi, go = operands[1], operands[6], operands[15], operands[16]
-    rows, model = normed.shape
+    hidden, q, gi, go, pick = operands[2], operands[8], operands[19], operands[20], operands[22]
+    rows, model = hidden.shape
     seq, local = q.shape
     heads = local // HDIM
     sems = chunk_sems(count)
+    small_rows = -(-(4 * model // 128 * pick.shape[0] + 2 * model // 128 + 16) // (16 * count)) * 16 * count
 
     def dma(n):
         return [pltpu.SemaphoreType.DMA((n,))] * 2
@@ -677,9 +669,15 @@
             pltpu.VMEM((rows, model), BF16),
         ] + dma(3 * PARTS)
 
-    scratch = scatter_scratch() + scatter_scratch()
-    scratch += [pltpu.VMEM((seq, model), BF16)] + dma(3 * PARTS)
+    scratch = scatter_scratch() + scatter_scratch() + scatter_scratch()
+    scratch += dma(3 * PARTS) + [pltpu.VMEM((3, 6 * model // 128, 128), F32)] + dma(3)
     scratch += [
+        pltpu.VMEM((seq, model), BF16),
+        pltpu.VMEM((rows, model), F32),
+        pltpu.VMEM((rows, model), F32),
+        pltpu.VMEM((seq, 3 * local), BF16),
+        pltpu.VMEM((6 * model // 128 + 16, 128), F32),
+        pltpu.VMEM((small_rows, 128), BF16),
         pltpu.VMEM((heads * rows, local), BF16),
         pltpu.VMEM((heads * rows, local), BF16),
         pltpu.VMEM((seq, heads * rows), BF16),
@@ -688,27 +686,27 @@
         pltpu.VMEM((seq, local), F32),
         pltpu.VMEM((seq // rows, local, rows), F32),
     ]
-    for grad in (gi, go):
+    for grad in (gi, go, gi):
         for _ in range(0, grad.shape[1], width):
             scratch += chunk_scratch(count, grad.shape[0], width) + dma(sems)
+    scratch += chunk_scratch(count, small_rows, 128) + dma(sems)
     shape = jax.ShapeDtypeStruct
     return pl.pallas_call(
         functools.partial(late_kernel, count, width),
         out_shape=[
-            shape((rows, model), F32),
-            shape((rows, model), F32),
-            shape((seq, model), BF16),
-            shape((seq, local), BF16),
-            shape((seq, local), BF16),
-            shape((seq, local), BF16),
+            shape((rows, model), BF16),
             shape((rows, model), F32),
             shape(gi.shape, BF16),
             shape(go.shape, BF16),
+            shape((model, 4 * local), BF16),
+            shape((small_rows, 128), BF16),
         ],
         in_specs=whole_vmem(len(operands)),
-        out_specs=whole_vmem(9),
+        out_specs=whole_vmem(6),
         scratch_shapes=scratch,
-        compiler_params=pltpu.CompilerParams(collective_id=cid, has_side_effects=True, vmem_limit_bytes=VMEM_LIMIT),
+        compiler_params=pltpu.CompilerParams(
+            collective_id=cid, has_side_effects=True, vmem_limit_bytes=67043328
+        ),
         name="late",
     )(*operands)
 
@@ -717,14 +715,6 @@
     centered = row_block - jnp.mean(row_block, axis=-1, keepdims=True)
     inverse = lax.rsqrt(jnp.mean(centered * centered, axis=-1, keepdims=True) + EPSILON)
     return (centered * inverse, inverse)
-
-
-def norm_back(grad_hat, normed, inverse):
-    return inverse * (
-        grad_hat
-        - jnp.mean(grad_hat, axis=-1, keepdims=True)
-        - normed * jnp.mean(grad_hat * normed, axis=-1, keepdims=True)
-    )
 
 
 def exact_gelu(values):
@@ -811,9 +801,7 @@
     grad_all = tensor_gather(cotangent, 4)
     inner_pre = dot(second_all, w_inner, ((1,), (0,))) + b_inner
     activated = exact_gelu(inner_pre).astype(BF16)
-    layer_out = (
-        hidden + tensor_scatter(dot(activated, w_outer, ((1,), (0,))).astype(BF16), 5) + b_outer
-    ).astype(BF16)
+    outer_part = dot(activated, w_outer, ((1,), (0,))).astype(BF16)
     grad_w_outer = dot(activated, grad_all, ((0,), (0,))).astype(BF16)
     grad_activated = dot(grad_all, w_outer, ((1,), (1,)))
     unused_value, gelu_pull = jax.vjp(exact_gelu, inner_pre)
@@ -824,25 +812,17 @@
     bias_keys = jnp.broadcast_to(jnp.where(valid_keys[0], 0.0, NEG_LARGE)[:, None], (SEQ, rows_dev))
     heads_here = w_query.shape[1] // HDIM
     logs = log_sums.reshape(heads_here, SEQ // rows_dev, rows_dev).transpose(1, 0, 2)
-    (
-        grad_second,
-        grad_hidden,
-        grad_attn_all,
-        grad_queries,
-        grad_keys,
-        grad_values,
-        grad_first,
-        sum_inner,
-        sum_outer,
-    ) = late(
+    layer_out, frames_grad, sum_inner, sum_outer, sum_attn, small = late(
         dp_count,
         512,
         6,
         second_part,
-        normed_two,
-        inverse_two,
+        outer_part,
+        hidden,
+        frames,
         cotangent,
-        gain[:, width:],
+        gain.reshape(2, width),
+        b_outer.reshape(1, width),
         w_out,
         queries,
         keys_all,
@@ -853,37 +833,13 @@
         w_query,
         w_key,
         w_value,
+        first_all,
+        attended,
         grad_w_inner,
         grad_w_outer,
+        grad_b_inner.reshape(-1, 128),
+        pick,
     )
-    grad_out_rows = cotangent.astype(F32)
-    grad_w_out = dot(grad_attn_all, attended, ((0,), (0,)))
-    grad_b_query = jnp.sum(grad_queries.astype(F32), axis=0)
-    grad_b_value = jnp.sum(grad_values.astype(F32), axis=0)
-    grad_w_attn = jnp.concatenate(
-        [
-            dot(first_all, grad_queries, ((0,), (0,))).astype(BF16),
-            dot(first_all, grad_keys, ((0,), (0,))).astype(BF16),
-            dot(first_all, grad_values, ((0,), (0,))).astype(BF16),
-            grad_w_out.astype(BF16),
-        ],
-        axis=1,
-    )
-    frames_grad = grad_hidden + norm_back(grad_first * gain[:, :width], normed_one, inverse_one)
-    vec = jnp.concatenate(
-        [
-            jnp.sum(grad_first * normed_one, axis=0),
-            jnp.sum(grad_second * normed_two, axis=0),
-            jnp.sum(grad_first, axis=0),
-            jnp.sum(grad_second, axis=0),
-            jnp.sum(grad_hidden, axis=0),
-            jnp.sum(grad_out_rows, axis=0),
-        ]
-    ).reshape(-1, 128)
-    bias = jnp.concatenate(
-        [grad_b_inner, grad_b_query, grad_b_value, jnp.zeros((2048 - 1024 - 512,), F32)]
-    ).reshape(16, 128)
-    sum_attn, small = dp_sum(dp_count, [grad_w_attn], [256], vec, bias, pick, 9)
     small = small.astype(F32)
     tables = small[: 32 * sections].reshape(sections, 2, 2 * width)
     shared = small[32 * sections : 32 * sections + 16].reshape(2, width)

time: 383 us -> 338 us (0.88)
  Pallas kernels: 266 us -> 234 us
  other arithmetic: 33.8 us -> 20.5 us
    pallas_call x1 -> x0, Pallas kernels: 63.7 us -> none  [dp_sum(): pl.pallas_call(functools.partial(dp_sum_kernel, count, tuple(widths)), ou...]
    pallas_call x1, Pallas kernels: 111 us -> 162 us  [late(): pl.pallas_call(functools.partial(late_kernel, count, width), out_shape=[s...]
    pallas_call x2 -> x1, Pallas kernels: 36.7 us -> 18.3 us  [tensor_scatter(): pl.pallas_call(scatter_kernel, out_shape=jax.ShapeDtypeStruct((rows, widt...]
    reduce_sum x6 -> x0, other arithmetic: 5.49 us -> none  [the longest x1 1.87 us: body(): jnp.sum(grad_second, axis=0)]
    unnamed x72 -> x61, local copies, waits for them, and re-layouts: 4.4 us -> 8.07 us
    dot_general x14 -> x10, matrix products: 47.1 us -> 45.7 us  [dot(): return lax.dot_general(a, b, (dims, ((), ())), preferred_element_type=F32)]
where the time goes in v3:
time: 338 us; the launch traced here: 334 us
  Pallas kernels  234 us (69%)
  matrix products  60.3 us (18%)
  other arithmetic  20.5 us (6%)
  local copies, waits for them, and re-layouts  16.6 us (5%)
    pallas_call x1, Pallas kernels, late(): pl.pallas_call(functools.partial(late_kernel, count, width), out_shape=[s...  162 us
    pallas_call x3, Pallas kernels, tensor_gather(): pl.pallas_call(gather_kernel, out_shape=jax.ShapeDtypeStruct((rows * 4, w...  54 us
    dot_general x10, matrix products, dot(): return lax.dot_general(a, b, (dims, ((), ())), preferred_element_type=F32)  45.7 us
    pallas_call x1, Pallas kernels, tensor_scatter(): pl.pallas_call(scatter_kernel, out_shape=jax.ShapeDtypeStruct((rows, widt...  18.3 us
    unnamed x61, local copies, waits for them, and re-layouts  8.07 us
    dot_general x2, matrix products, masked_scores(): jnp.einsum('sqhe,skhe->shqk', query_block, keys_all, preferred_element_ty...  7.35 us
    dot_general x2, matrix products, attention_forward(): jnp.einsum('shqk,skhe->sqhe', softmax_low, values_all, preferred_element_...  7.27 us

profile of v3, /device:TPU:0, one launch (start us, length us, event | category | flops | bytes accessed | tf_op | source)
XLA Modules:
  0.0 334.4 jit_solution(13730191732270150376)
XLA Ops:
  1.4 0.9 fusion.37
  2.3 1.2 convert_reduce_fusion.1
  3.5 1.3 fusion.20
  4.9 2.1 fusion.23.x_ref
  7.0 19.1 %tensor_gather_1.1.refs_17_ = bf16[1024,1024]{1,0:T(8,128)(2,1)} custom-call(bf16[256,1024]{1,0:T(8,128)(2,1)} %fusion.23.x_ref), custom_call_target="tpu_custom_call" | custom-call | tf_op jit(solution)/shard_map/tensor_gather_1/pallas_call | solution.py:79
  26.1 2.3 convolution_convert_fusion.5
  28.4 2.5 fusion.13.refs_8_
  31.8 1.4 fusion
  33.3 5.9 %fusion.2 = (f32[4,512]{1,0:T(4,128)S(1)}, f32[4,512]{1,0:T(4,128)S(1)}, f32[4,512,1024]{2,1,0:T(8,128)}) fusion(f32[4,512,1024]{2,1,0:T(8,128)S(1)} %get-tuple-element.82, f32[4,512]{1,0:T(4,128)S(1)} %get-tuple-element.81, pred[1024]{0:T(1024)(128)(4,1)S(1)} %get-tuple-element.63, bf16[1024,4,64]{0,2,1:T(8,128)(2,1)S(1)} %bitcast.85, ...), kind=kOutput, calls=%fused_computation.8 | convolution fusion | flops 283111424 | bytes 17589248 | tf_op jit(solution)/shard_map/sqhe,skhe->shqk/dot_general | solution.py:733
  39.2 0.3 copy-done.3
  39.5 0.7 fusion.12.refs_11_
  40.5 4.8 %fusion.18 = bf16[1,512,4,64]{1,3,2,0:T(8,128)(2,1)S(1)} fusion(bf16[1024,4,64]{0,2,1:T(8,128)(2,1)S(1)} %bitcast.91, f32[4,512,1024]{2,1,0:T(8,128)} %copy-done.3, f32[4,512]{1,0:T(4,128)S(1)} %get-tuple-element.57, f32[4,512]{1,0:T(4,128)S(1)} %get-tuple-element.81, pred[1024]{0:T(1024)(128)(4,1)S(1)} %get-tuple-element.63), kind=kOutput, calls=%fused_computation.47 | convolution fusion | flops 279052288 | bytes 9192448 | tf_op jit(solution)/shard_map/shqk,skhe->sqhe/dot_general | solution.py:746
  45.3 1.1 slice-done.1
  46.4 2.0 fusion.3
  48.4 2.5 fusion.19
  51.0 2.1 convolution_convert_fusion.4.p_ref
  53.1 18.3 %tensor_scatter_2.1 = f32[256,1024]{1,0:T(8,128)} custom-call(bf16[1024,1024]{1,0:T(8,128)(2,1)} %convolution_convert_fusion.4.p_ref), custom_call_target="tpu_custom_call" | custom-call | tf_op jit(solution)/shard_map/tensor_scatter_2/pallas_call | solution.py:131
  71.4 1.4 fusion.34
  73.1 0.7 copy-done
  73.8 1.0 add_convert_fusion.1.x_ref
  74.9 17.2 %tensor_gather_3.1 = bf16[1024,1024]{1,0:T(8,128)(2,1)} custom-call(bf16[256,1024]{1,0:T(8,128)(2,1)} %add_convert_fusion.1.x_ref), custom_call_target="tpu_custom_call" | custom-call | tf_op jit(solution)/shard_map/tensor_gather_3/pallas_call | solution.py:79
  92.1 6.7 %fusion.39 = f32[1024,1024]{1,0:T(8,128)} fusion(bf16[1024,1024]{1,0:T(8,128)(2,1)} %tensor_gather_3.1, bf16[1024,1024]{1,0:T(8,128)(2,1)} %param.29), kind=kOutput, calls=%fused_computation.94 | convolution fusion | flops 2147483648 | bytes 8388608 | tf_op jit(solution)/shard_map/dot_general | solution.py:729
  98.8 17.7 %tensor_gather_4.1 = bf16[1024,1024]{1,0:T(8,128)(2,1)} custom-call(bf16[256,1024]{1,0:T(8,128)(2,1)} %refs_4_.1), custom_call_target="tpu_custom_call" | custom-call | tf_op jit(solution)/shard_map/tensor_gather_4/pallas_call | solution.py:79
  116.5 14.8 %convert_reduce_fusion = (f32[1024]{0:T(1024)}, bf16[1024,1024]{1,0:T(8,128)(2,1)S(1)}, f32[1024,1024]{1,0:T(8,128)S(1)}) fusion(f32[1024,1024]{1,0:T(8,128)} %fusion.39, f32[1024]{0:T(1024)S(1)} %copy-done.18, bf16[1024,1024]{1,0:T(8,128)(2,1)} %tensor_gather_4.1, bf16[1024,1024]{1,0:T(8,128)(2,1)S(1)} %copy-done.20), kind=kOutput, calls=%fused_computation.12 | convolution fusion | flops 2226125824 | bytes 14688256 | tf_op jit(solution)/shard_map/dot_general | solution.py:729
  131.3 3.8 %convolution_convert_fusion.1.refs_19_ = bf16[1024,1024]{1,0:T(8,128)(2,1)} fusion(bf16[1024,1024]{1,0:T(8,128)(2,1)S(1)} %copy-done.8, bf16[1024,1024]{1,0:T(8,128)(2,1)S(1)} %get-tuple-element.60), kind=kOutput, calls=%fused_computation.31 | convolution fusion | flops 2148532224 | bytes 6291456 | tf_op jit(solution)/shard_map/dot_general | solution.py:729
  135.1 1.2 multiply_convert_fusion
  136.3 0.4 copy-done.7
  136.7 3.7 %convolution_convert_fusion.refs_20_ = bf16[1024,1024]{1,0:T(8,128)(2,1)} fusion(bf16[1024,1024]{1,0:T(8,128)(2,1)S(1)} %multiply_convert_fusion, bf16[1024,1024]{1,0:T(8,128)(2,1)S(1)} %copy-done.7), kind=kOutput, calls=%fused_computation.30 | convolution fusion | flops 2148532224 | bytes 6291456 | tf_op jit(solution)/shard_map/dot_general | solution.py:729
  140.5 0.6 reshape.227.refs_12_
  141.1 5.4 %convolution_convert_fusion.2.refs_1_ = bf16[1024,1024]{1,0:T(8,128)(2,1)} fusion(bf16[1024,1024]{1,0:T(8,128)(2,1)S(1)} %multiply_convert_fusion, bf16[1024,1024]{1,0:T(8,128)(2,1)} %param.31), kind=kOutput, calls=%fused_computation.32 | convolution fusion | flops 2148532224 | bytes 6291456 | tf_op jit(solution)/shard_map/dot_general | solution.py:729
  146.5 3.7 %convolution_convert_fusion.3.refs_0_ = bf16[1024,1024]{1,0:T(8,128)(2,1)} fusion(bf16[1024,1024]{1,0:T(8,128)(2,1)S(1)} %copy-done.25, bf16[1024,1024]{1,0:T(8,128)(2,1)S(1)} %copy-done.21), kind=kOutput, calls=%fused_computation.33 | convolution fusion | flops 2148532224 | bytes 6291456 | tf_op jit(solution)/shard_map/dot_general | solution.py:729
  150.2 1.0 copy.49.refs_18_
  151.2 1.0 copy.48.refs_9_
  152.2 0.9 dynamic-slice_reduce_fusion
  153.1 0.6 reshape.224.refs_5_
  153.7 0.7 broadcast_in_dim.33.refs_22_
  154.3 1.2 broadcast_in_dim.32.refs_13_
  155.5 162.0 %late.1 = (bf16[256,1024]{1,0:T(8,128)(2,1)}, f32[256,1024]{1,0:T(8,128)}, bf16[1024,1024]{1,0:T(8,128)(2,1)}, bf16[1024,1024]{1,0:T(8,128)(2,1)}, bf16[1024,1024]{1,0:T(8,128)(2,1)}, /*index=5*/bf16[256,128]{1,0:T(8,128)(2,1)}) custom-call(bf16[1024,1024]{1,0:T(8,128)(2,1)} %convolution_convert_fusion.3.refs_0_, ...), custom_call_target="tpu_custom_call" | custom-call | tf_op jit(solution)/shard_map/late/pallas_call | solution.py:694
  317.5 3.3 convert_bitcast_fusion
  320.8 1.3 copy.52
  322.1 4.1 %convert_element_type.131 = f32[1024,1024]{1,0:T(8,128)} convert(bf16[1024,1024]{1,0:T(8,128)(2,1)} %get-tuple-element.25) | non-fusion elementwise | flops 1048576 | bytes 6291456 | tf_op jit(solution)/shard_map/convert_element_type | solution.py:861
  326.2 2.5 convert_element_type.132
  328.9 0.7 copy.59
  329.5 0.7 copy.60
  330.2 0.6 slice_bitcast_fusion.4
  330.8 0.6 slice_bitcast_fusion.7
  331.4 1.9 copy.65
  333.2 1.0 copy.66
  (70 shorter events, 1.1 us)
Async XLA Ops:
  0.6 25.4 %copy-start.14 = (bf16[1024,256]{1,0:T(8,128)(2,1)S(1)}, bf16[1024,256]{1,0:T(8,128)(2,1)}, u32[]{:S(2)}) copy-start(bf16[1024,256]{1,0:T(8,128)(2,1)} %refs_15_.1) | copy-start | bytes 1572868
  0.7 27.8 %copy-start.15 = (bf16[1024,256]{1,0:T(8,128)(2,1)S(1)}, bf16[1024,256]{1,0:T(8,128)(2,1)}, u32[]{:S(2)}) copy-start(bf16[1024,256]{1,0:T(8,128)(2,1)} %refs_14_.1) | copy-start | bytes 1572868
  0.7 27.8 %copy-start.22 = (f32[256]{0:T(256)S(1)}, f32[256]{0:T(256)}, u32[]{:S(2)}) copy-start(f32[256]{0:T(256)} %param.23) | copy-start | bytes 3076
  28.4 122.8 %copy-start.4 = (bf16[1024,256]{0,1:T(8,128)(2,1)}, bf16[1024,256]{0,1:T(8,128)(2,1)S(1)}, u32[]{:S(2)}) copy-start(bf16[1024,256]{0,1:T(8,128)(2,1)S(1)} %convolution_convert_fusion.5) | copy-start | bytes 1572868
  28.4 3.4 %copy-start.19 = (s32[1024]{0:T(1024)S(1)}, s32[1024]{0:T(1024)}, u32[]{:S(2)}) copy-start(s32[1024]{0:T(1024)} %param.35) | copy-start | bytes 12292
  30.9 2.3 copy-start.9
  33.2 6.3 %copy-start.3 = (f32[4,512,1024]{2,1,0:T(8,128)}, f32[4,512,1024]{2,1,0:T(8,128)S(1)}, u32[]{:S(2)}) copy-start(f32[4,512,1024]{2,1,0:T(8,128)S(1)} %get-tuple-element.82) | copy-start | bytes 25165828
  33.2 6.3 %copy-start.2 = (bf16[1024,1024]{1,0:T(8,128)(2,1)S(1)}, bf16[1024,1024]{1,0:T(8,128)(2,1)}, u32[]{:S(2)}) copy-start(bf16[1024,1024]{1,0:T(8,128)(2,1)} %tensor_gather_1.1.refs_17_) | copy-start | bytes 6291460
  33.3 6.3 %copy-start.13 = (bf16[1024,256]{1,0:T(8,128)(2,1)S(1)}, bf16[1024,256]{1,0:T(8,128)(2,1)}, u32[]{:S(2)}) copy-start(bf16[1024,256]{1,0:T(8,128)(2,1)} %refs_16_.1) | copy-start | bytes 1572868
  33.3 6.3 %copy-start.23 = (f32[256]{0:T(256)S(1)}, f32[256]{0:T(256)}, u32[]{:S(2)}) copy-start(f32[256]{0:T(256)} %param.26) | copy-start | bytes 3076
  40.2 5.0 %copy-start.10 = (bf16[1024,256]{1,0:T(8,128)(2,1)}, bf16[1024,256]{1,0:T(8,128)(2,1)S(1)}, u32[]{:S(2)}) copy-start(bf16[1024,256]{1,0:T(8,128)(2,1)S(1)} %fusion.12.refs_11_) | copy-start | bytes 1572868
  40.5 4.8 %slice-start = ((s8[8388608]{0:T(1024)(128)(4,1)}), s8[4194304]{0:T(1024)(128)(4,1)S(1)}, s32[]{:S(2)}) async-start(s8[8388608]{0:T(1024)(128)(4,1)} %bitcast.82), calls=%async_computation | async-start | bytes 8388608
  40.5 5.9 %slice-start.1 = ((s8[8388608]{0:T(1024)(128)(4,1)}), s8[4194304]{0:T(1024)(128)(4,1)S(1)}, s32[]{:S(2)}) async-start(s8[8388608]{0:T(1024)(128)(4,1)} %bitcast.82), calls=%async_computation.1 | async-start | bytes 8388608
  48.4 2.6 copy-start.11
  50.9 20.5 %copy-start.1 = (bf16[256,1024]{1,0:T(8,128)(2,1)S(1)}, bf16[256,1024]{1,0:T(8,128)(2,1)}, u32[]{:S(2)}) copy-start(bf16[256,1024]{1,0:T(8,128)(2,1)} %refs_3_.1) | copy-start | bytes 1572868
  50.9 20.5 %copy-start.17 = (f32[1024]{0:T(1024)S(1)}, f32[1024]{0:T(1024)}, u32[]{:S(2)}) copy-start(f32[1024]{0:T(1024)} %param.28) | copy-start | bytes 12292
  72.8 1.0 copy-start
  92.1 24.4 %copy-start.18 = (f32[1024]{0:T(1024)S(1)}, f32[1024]{0:T(1024)}, u32[]{:S(2)}) copy-start(f32[1024]{0:T(1024)} %param.30) | copy-start | bytes 12292
  92.1 24.4 %copy-start.20 = (bf16[1024,1024]{1,0:T(8,128)(2,1)S(1)}, bf16[1024,1024]{1,0:T(8,128)(2,1)}, u32[]{:S(2)}) copy-start(bf16[1024,1024]{1,0:T(8,128)(2,1)} %param.31) | copy-start | bytes 6291460
  116.5 14.8 %copy-start.8 = (bf16[1024,1024]{1,0:T(8,128)(2,1)S(1)}, bf16[1024,1024]{1,0:T(8,128)(2,1)}, u32[]{:S(2)}) copy-start(bf16[1024,1024]{1,0:T(8,128)(2,1)} %tensor_gather_3.1) | copy-start | bytes 6291460
  131.3 3.8 %copy-start.24 = (bf16[1024,1024]{1,0:T(8,128)(2,1)}, bf16[1024,1024]{1,0:T(8,128)(2,1)S(1)}, u32[]{:S(2)}) copy-start(bf16[1024,1024]{1,0:T(8,128)(2,1)S(1)} %get-tuple-element.60) | copy-start | bytes 6291460
  131.3 3.8 %copy-start.5 = (f32[1024,1024]{1,0:T(8,128)S(1)}, f32[1024,1024]{1,0:T(8,128)}, u32[]{:S(2)}) copy-start(f32[1024,1024]{1,0:T(8,128)} %fusion.39) | copy-start | bytes 12582916
  135.1 1.6 copy-start.7
  141.1 5.4 %copy-start.21 = (bf16[1024,1024]{1,0:T(8,128)(2,1)S(1)}, bf16[1024,1024]{1,0:T(8,128)(2,1)}, u32[]{:S(2)}) copy-start(bf16[1024,1024]{1,0:T(8,128)(2,1)} %param.29) | copy-start | bytes 6291460
  141.1 5.4 %copy-start.25 = (bf16[1024,1024]{1,0:T(8,128)(2,1)S(1)}, bf16[1024,1024]{1,0:T(8,128)(2,1)}, u32[]{:S(2)}) copy-start(bf16[1024,1024]{1,0:T(8,128)(2,1)} %copy-done.24) | copy-start | bytes 6291460
  320.8 5.4 %copy-start.6 = (bf16[1024,1024]{1,0:T(8,128)(2,1)S(1)}, bf16[1024,1024]{1,0:T(8,128)(2,1)}, u32[]{:S(2)}) copy-start(bf16[1024,1024]{1,0:T(8,128)(2,1)} %get-tuple-element.26) | copy-start | bytes 6291460
  326.2 2.5 copy-start.16
  326.2 7.0 %copy-start.12 = (f32[256,1024]{1,0:T(8,128)S(1)}, f32[256,1024]{1,0:T(8,128)}, u32[]{:S(2)}) copy-start(f32[256,1024]{1,0:T(8,128)} %get-tuple-element.102) | copy-start | bytes 3145732

commit v4 on v3

--- a/solution.py
+++ b/solution.py
@@ -44,105 +44,6 @@
 
 
 PARTS = 4
-
-
-def gather_kernel(x_ref, o_ref, send, recv):
-    dp, me, sib, across, diag = places()
-    rows = x_ref.shape[0]
-    part = rows // PARTS
-    greet([(dp, sib), (dp, across)])
-    copies = []
-    for i in range(PARTS):
-        at = pl.multiple_of(me * rows + i * part, part)
-        copies.append(
-            remote(x_ref.at[pl.ds(i * part, part)], o_ref.at[pl.ds(at, part)], send.at[i], recv.at[i], (dp, across))
-        )
-        copies[-1].start()
-    mine = pl.ds(pl.multiple_of(me * rows, rows), rows)
-    copies.append(remote(x_ref, o_ref.at[mine], send.at[PARTS], recv.at[PARTS], (dp, sib)))
-    copies[-1].start()
-    o_ref[mine, :] = x_ref[...]
-    for i in range(PARTS):
-        copies[i].wait_recv()
-        there = pl.ds(pl.multiple_of(across * rows + i * part, part), part)
-        j = PARTS + 1 + i
-        copies.append(remote(o_ref.at[there], o_ref.at[there], send.at[j], recv.at[j], (dp, sib)))
-        copies[-1].start()
-    for i, copy in enumerate(copies):
-        if i >= PARTS:
-            copy.wait_recv()
-        copy.wait_send()
-
-
-def tensor_gather(block, cid):
-    rows, width = block.shape
-    return pl.pallas_call(
-        gather_kernel,
-        out_shape=jax.ShapeDtypeStruct((rows * 4, width), block.dtype),
-        in_specs=whole_vmem(1),
-        out_specs=pl.BlockSpec(memory_space=pltpu.VMEM),
-        scratch_shapes=[pltpu.SemaphoreType.DMA((2 * PARTS + 1,))] * 2,
-        compiler_params=pltpu.CompilerParams(collective_id=cid, has_side_effects=True, vmem_limit_bytes=VMEM_LIMIT),
-        name="tensor_gather_%d" % cid,
-    )(block)
-
-
-def scatter_kernel(p_ref, o_ref, from_sib, chip_sum, landed, send, recv):
-    dp, me, sib, across, diag = places()
-    rows = p_ref.shape[0] // 4
-    part = rows // PARTS
-    greet([(dp, sib), (dp, across)])
-
-    def at(owner, i):
-        return pl.ds(pl.multiple_of(owner * rows + i * part, part), part)
-
-    first, last = [], []
-    for i in range(PARTS):
-        here = pl.ds(i * part, part)
-        first.append(remote(p_ref.at[at(diag, i)], from_sib.at[0, here], send.at[i], recv.at[i], (dp, sib)))
-        first[-1].start()
-    for i in range(PARTS):
-        here = pl.ds(i * part, part)
-        j = PARTS + i
-        last.append(remote(p_ref.at[at(sib, i)], from_sib.at[1, here], send.at[j], recv.at[j], (dp, sib)))
-        last[-1].start()
-    crossing = []
-    for i in range(PARTS):
-        here = pl.ds(i * part, part)
-        j = 2 * PARTS + i
-        first[i].wait_recv()
-        chip_sum[here, :] = (p_ref[at(across, i), :].astype(F32) + from_sib[0, here, :].astype(F32)).astype(BF16)
-        crossing.append(remote(chip_sum.at[here], landed.at[here], send.at[j], recv.at[j], (dp, across)))
-        crossing[-1].start()
-    for i in range(PARTS):
-        here = pl.ds(i * part, part)
-        last[i].wait_recv()
-        o_ref[here, :] = p_ref[at(me, i), :].astype(F32) + from_sib[1, here, :].astype(F32)
-    for i in range(PARTS):
-        here = pl.ds(i * part, part)
-        crossing[i].wait_recv()
-        o_ref[here, :] = o_ref[here, :] + landed[here, :].astype(F32)
-    for copy in first + last + crossing:
-        copy.wait_send()
-
-
-def tensor_scatter(partial, cid):
-    rows, width = partial.shape[0] // 4, partial.shape[1]
-    return pl.pallas_call(
-        scatter_kernel,
-        out_shape=jax.ShapeDtypeStruct((rows, width), F32),
-        in_specs=whole_vmem(1),
-        out_specs=pl.BlockSpec(memory_space=pltpu.VMEM),
-        scratch_shapes=[
-            pltpu.VMEM((2, rows, width), BF16),
-            pltpu.VMEM((rows, width), BF16),
-            pltpu.VMEM((rows, width), BF16),
-            pltpu.SemaphoreType.DMA((3 * PARTS,)),
-            pltpu.SemaphoreType.DMA((3 * PARTS,)),
-        ],
-        compiler_params=pltpu.CompilerParams(collective_id=cid, has_side_effects=True, vmem_limit_bytes=VMEM_LIMIT),
-        name="tensor_scatter_%d" % cid,
-    )(partial)
 
 
 def dp_lines(count):
@@ -398,6 +299,44 @@
 
     def finish(self):
         for copy in self.first + self.last + self.crossing:
+            copy.wait_send()
+
+
+class Gather:
+    def __init__(self, spot, all_ref, send, recv):
+        self.dp, self.me, self.sib, self.across, self.diag = spot
+        self.rows = all_ref.shape[0] // 4
+        self.part = self.rows // PARTS
+
+        def copy(owner, i, slot, device):
+            ref = all_ref.at[self.at(owner, i)]
+            return remote(ref, ref, send.at[slot], recv.at[slot], (self.dp, device))
+
+        self.to_across = [copy(self.me, i, i, self.across) for i in range(PARTS)]
+        self.to_sib = [copy(self.me, i, PARTS + i, self.sib) for i in range(PARTS)]
+        self.passed = [copy(self.across, i, 2 * PARTS + i, self.sib) for i in range(PARTS)]
+
+    def at(self, owner, i):
+        return pl.ds(pl.multiple_of(owner * self.rows + i * self.part, self.part), self.part)
+
+    def start(self, i):
+        self.to_across[i].start()
+        self.to_sib[i].start()
+
+    def pass_on(self, i):
+        self.to_across[i].wait_recv()
+        self.passed[i].start()
+
+    def wait_sib(self):
+        for copy in self.to_sib:
+            copy.wait_recv()
+
+    def wait_diag(self):
+        for copy in self.passed:
+            copy.wait_recv()
+
+    def finish(self):
+        for copy in self.to_across + self.to_sib + self.passed:
             copy.wait_send()
 
 
@@ -711,42 +650,153 @@
     )(*operands)
 
 
-def normalize(row_block):
-    centered = row_block - jnp.mean(row_block, axis=-1, keepdims=True)
-    inverse = lax.rsqrt(jnp.mean(centered * centered, axis=-1, keepdims=True) + EPSILON)
-    return (centered * inverse, inverse)
+def front_kernel(*refs):
+    frames_ref, cot_ref, gain_ref, shift_ref, wq_ref, bq_ref, wk_ref, wv_ref, bv_ref = refs[:9]
+    bias_ref, w_out_ref, b_out_ref = refs[9:12]
+    first_ref, call_ref, q_ref, k_ref, kt_ref, v_ref, log_ref, att_ref, hidden_ref, second_ref = refs[12:22]
+    total_ref, vt_ref, q_cat, att_t, from_sib, chip_sum, landed = refs[22:29]
+    ssend, srecv, asend, arecv, csend, crecv, bsend, brecv = refs[29:]
+    spot = places()
+    dp, me, sib, across, diag = spot
+    greet([(dp, sib), (dp, across)])
+    rows = frames_ref.shape[0]
+    part = rows // PARTS
+    local = q_ref.shape[1]
+    heads = local // HDIM
+    scale = HDIM ** (-0.5)
+    firsts = Gather(spot, first_ref, asend, arecv)
+    cots = Gather(spot, call_ref, csend, crecv)
+    seconds = Gather(spot, second_ref, bsend, brecv)
+    for i in range(PARTS):
+        here = pl.ds(i * part, part)
+        normed, _ = norm_parts(frames_ref[here, :].astype(F32))
+        first_ref[firsts.at(me, i), :] = (normed * gain_ref[0:1, :] + shift_ref[0:1, :]).astype(BF16)
+        firsts.start(i)
+    for i in range(PARTS):
+        call_ref[cots.at(me, i), :] = cot_ref[pl.ds(i * part, part), :]
+        cots.start(i)
+
+    def project(owner):
+        block = pl.ds(pl.multiple_of(owner * rows, rows), rows)
+        x = first_ref[block, :]
+        q_ref[block, :] = (dot(x, wq_ref[...], ((1,), (0,))) + bq_ref[...]).astype(BF16)
+        keys = dot(x, wk_ref[...], ((1,), (0,)))
+        k_ref[block, :] = keys.astype(BF16)
+        kt_ref[:, block] = keys.T.astype(BF16)
+        values = dot(x, wv_ref[...], ((1,), (0,))) + bv_ref[...]
+        v_ref[block, :] = values.astype(BF16)
+        vt_ref[:, block] = values.T.astype(BF16)
+
+    project(me)
+    firsts.wait_sib()
+    firsts.pass_on(0)
+    firsts.pass_on(1)
+    project(sib)
+    firsts.pass_on(2)
+    firsts.pass_on(3)
+    project(across)
+    firsts.wait_diag()
+    project(diag)
+
+    lanes = lax.broadcasted_iota(jnp.int32, (rows, local), 1) // HDIM
+
+    def attend(owner):
+        block = pl.ds(pl.multiple_of(owner * rows, rows), rows)
+        query = q_ref[block, :]
+        for h in range(heads):
+            q_cat[pl.ds(h * rows, rows), :] = jnp.where(lanes == h, query, jnp.zeros_like(query))
+
+        @pl.loop(0, heads, step=2)
+        def _(pair):
+            for h in (pair, pair + 1):
+                at = pl.ds(pl.multiple_of(h * rows, rows), rows)
+                scores = dot(k_ref[...], q_cat[at, :], ((1,), (1,))) * scale + bias_ref[...]
+                highest = jnp.max(scores, axis=0, keepdims=True)
+                weights = jnp.exp(scores - highest)
+                sums = jnp.sum(weights, axis=0, keepdims=True)
+                low = (weights * (1.0 / sums)).astype(BF16)
+                head = pl.ds(pl.multiple_of(h * HDIM, HDIM), HDIM)
+                att_t[head, :] = dot(vt_ref[head, :], low, ((1,), (0,)))
+                log_ref[owner * heads + h] = highest + jnp.log(sums)
+
+        attended = att_t[...].T.astype(BF16)
+        att_ref[block, :] = attended
+        total_ref[block, :] = dot(attended, w_out_ref[...], ((1,), (0,))).astype(BF16)
+
+    sums = Scatter(spot, total_ref, from_sib, chip_sum, landed, ssend, srecv)
+    attend(diag)
+    sums.start_first()
+    attend(across)
+    sums.cross()
+    attend(sib)
+    sums.start_last()
+    attend(me)
+    for i in range(PARTS):
+        here = pl.ds(i * part, part)
+        hidden = frames_ref[here, :].astype(F32) + sums.result(i) + b_out_ref[...]
+        hidden_ref[here, :] = hidden
+        normed, _ = norm_parts(hidden)
+        second_ref[seconds.at(me, i), :] = (normed * gain_ref[1:2, :] + shift_ref[1:2, :]).astype(BF16)
+        seconds.start(i)
+    for i in range(PARTS):
+        cots.pass_on(i)
+    for i in range(PARTS):
+        seconds.pass_on(i)
+    cots.wait_sib()
+    cots.wait_diag()
+    seconds.wait_sib()
+    seconds.wait_diag()
+    firsts.finish()
+    cots.finish()
+    sums.finish()
+    seconds.finish()
+
+
+def front(cid, *operands):
+    frames, wq = operands[0], operands[4]
+    rows, model = frames.shape
+    local = wq.shape[1]
+    heads = local // HDIM
+    shape = jax.ShapeDtypeStruct
+    return pl.pallas_call(
+        front_kernel,
+        out_shape=[
+            shape((4 * rows, model), BF16),
+            shape((4 * rows, model), BF16),
+            shape((4 * rows, local), BF16),
+            shape((4 * rows, local), BF16),
+            shape((local, 4 * rows), BF16),
+            shape((4 * rows, local), BF16),
+            shape((4 * heads, 1, rows), F32),
+            shape((4 * rows, local), BF16),
+            shape((rows, model), F32),
+            shape((4 * rows, model), BF16),
+        ],
+        in_specs=whole_vmem(len(operands)),
+        out_specs=whole_vmem(10),
+        scratch_shapes=[
+            pltpu.VMEM((4 * rows, model), BF16),
+            pltpu.VMEM((local, 4 * rows), BF16),
+            pltpu.VMEM((heads * rows, local), BF16),
+            pltpu.VMEM((local, rows), F32),
+            pltpu.VMEM((2, rows, model), BF16),
+            pltpu.VMEM((rows, model), BF16),
+            pltpu.VMEM((rows, model), BF16),
+        ]
+        + [pltpu.SemaphoreType.DMA((3 * PARTS,))] * 8,
+        compiler_params=pltpu.CompilerParams(
+            collective_id=cid, has_side_effects=True, vmem_limit_bytes=VMEM_LIMIT
+        ),
+        name="front",
+    )(*operands)
 
 
 def exact_gelu(values):
     return jax.nn.gelu(values, approximate=False)
 
 
-def split_heads(flat_rows):
-    return flat_rows.reshape(-1, SEQ, flat_rows.shape[1] // HDIM, HDIM)
-
-
 def dot(a, b, dims):
     return lax.dot_general(a, b, (dims, ((), ())), preferred_element_type=F32)
-
-
-def masked_scores(query_block, keys_all, valid_keys, score_scale):
-    scores = jnp.einsum("sqhe,skhe->shqk", query_block, keys_all, preferred_element_type=F32) * score_scale
-    return jnp.where(valid_keys[:, None, None, :], scores, NEG_LARGE)
-
-
-def attention_forward(queries, keys_all, values_all, valid_keys, score_scale, block_rows):
-    pieces = []
-    log_sums = []
-    for offset in range(0, SEQ, block_rows):
-        scores = masked_scores(queries[:, offset : offset + block_rows], keys_all, valid_keys, score_scale)
-        highest = jnp.max(scores, axis=-1, keepdims=True)
-        weights = jnp.exp(scores - highest)
-        totals = jnp.sum(weights, axis=-1, keepdims=True)
-        softmax_low = (weights / totals).astype(BF16)
-        mixture = jnp.einsum("shqk,skhe->sqhe", softmax_low, values_all, preferred_element_type=F32)
-        pieces.append(mixture.astype(BF16))
-        log_sums.append((highest + jnp.log(totals))[..., 0])
-    return (jnp.concatenate(pieces, axis=1), jnp.concatenate(log_sums, axis=2))
 
 
 def body(
@@ -773,8 +823,6 @@
     rows_dev, width = frames.shape
     sections = ada_gain.shape[0]
     assert section_index.shape[0] == 1
-    score_scale = HDIM ** (-0.5)
-    block_rows = 512
     section = section_index[0] - 2
     gain = lax.dynamic_slice(ada_gain, (section, 0), (1, 2 * width))
     shift = lax.dynamic_slice(ada_shift, (section, 0), (1, 2 * width))
@@ -783,22 +831,22 @@
     )
     spots = jnp.arange(SEQ, dtype=jnp.int32)
     valid_keys = (spots[None, :] < lengths[:, None]) & (key_mask.reshape(1, SEQ) > 0)
-    inputs = frames.astype(F32)
-    normed_one, inverse_one = normalize(inputs)
-    first_low = (normed_one * gain[:, :width] + shift[:, :width]).astype(BF16)
-    first_all = tensor_gather(first_low, 1)
-    queries = (dot(first_all, w_query, ((1,), (0,))) + b_query).astype(BF16)
-    keys_all = dot(first_all, w_key, ((1,), (0,))).astype(BF16)
-    values_all = (dot(first_all, w_value, ((1,), (0,))) + b_value).astype(BF16)
-    attended_heads, log_sums = attention_forward(
-        split_heads(queries), split_heads(keys_all), split_heads(values_all), valid_keys, score_scale, block_rows
+    bias_keys = jnp.broadcast_to(jnp.where(valid_keys[0], 0.0, NEG_LARGE)[:, None], (SEQ, rows_dev))
+    first_all, grad_all, queries, keys_all, keys_turned, values_all, logs, attended, hidden, second_all = front(
+        1,
+        frames,
+        cotangent,
+        gain.reshape(2, width),
+        shift.reshape(2, width),
+        w_query,
+        b_query.reshape(1, -1),
+        w_key,
+        w_value,
+        b_value.reshape(1, -1),
+        bias_keys,
+        w_out,
+        b_out.reshape(1, width),
     )
-    attended = attended_heads.reshape(queries.shape)
-    hidden = inputs + tensor_scatter(dot(attended, w_out, ((1,), (0,))).astype(BF16), 2) + b_out
-    normed_two, inverse_two = normalize(hidden)
-    second_low = (normed_two * gain[:, width:] + shift[:, width:]).astype(BF16)
-    second_all = tensor_gather(second_low, 3)
-    grad_all = tensor_gather(cotangent, 4)
     inner_pre = dot(second_all, w_inner, ((1,), (0,))) + b_inner
     activated = exact_gelu(inner_pre).astype(BF16)
     outer_part = dot(activated, w_outer, ((1,), (0,))).astype(BF16)
@@ -809,9 +857,6 @@
     grad_w_inner = dot(second_all, grad_inner, ((0,), (0,))).astype(BF16)
     grad_b_inner = jnp.sum(grad_inner.astype(F32), axis=0)
     second_part = dot(grad_inner, w_inner, ((1,), (1,))).astype(BF16)
-    bias_keys = jnp.broadcast_to(jnp.where(valid_keys[0], 0.0, NEG_LARGE)[:, None], (SEQ, rows_dev))
-    heads_here = w_query.shape[1] // HDIM
-    logs = log_sums.reshape(heads_here, SEQ // rows_dev, rows_dev).transpose(1, 0, 2)
     layer_out, frames_grad, sum_inner, sum_outer, sum_attn, small = late(
         dp_count,
         512,
@@ -826,9 +871,9 @@
         w_out,
         queries,
         keys_all,
-        keys_all.T,
+        keys_turned,
         values_all,
-        logs.reshape(-1, 1, rows_dev),
+        logs,
         bias_keys,
         w_query,
         w_key,

time: 338 us -> 282 us (0.83)
  matrix products: 60.3 us -> 31.8 us
  Pallas kernels: 234 us -> 222 us
  other arithmetic: 20.5 us -> 11.7 us
  local copies, waits for them, and re-layouts: 16.6 us -> 10.8 us
    dot_general x4 -> x0, matrix products: 14.6 us -> none  [the longest x2 7.35 us: masked_scores(): jnp.einsum('sqhe,skhe->shqk', query_block, keys_all, preferred_element_ty...]
    dot_general x10 -> x6, matrix products: 45.7 us -> 31.8 us  [dot(): return lax.dot_general(a, b, (dims, ((), ())), preferred_element_type=F32)]
    pallas_call x4 -> x1, Pallas kernels: 72.3 us -> 59.6 us  [front(): pl.pallas_call(front_kernel, out_shape=[shape((4 * rows, model), BF16), s...]
    reduce_sum x5 -> x0, other arithmetic: 6.22 us -> none  [the longest x2 2.64 us: normalize(): centered = row_block - jnp.mean(row_block, axis=-1, keepdims=True)]
    unnamed x61 -> x21, local copies, waits for them, and re-layouts: 8.07 us -> 5.48 us
where the time goes in v4:
time: 282 us; the launch traced here: 279 us
  Pallas kernels  222 us (79%)
  matrix products  31.8 us (11%)
  other arithmetic  11.7 us (4%)
  local copies, waits for them, and re-layouts  10.8 us (4%)
    pallas_call x1, Pallas kernels, late(): pl.pallas_call(functools.partial(late_kernel, count, width), out_shape=[s...  163 us
    pallas_call x1, Pallas kernels, front(): pl.pallas_call(front_kernel, out_shape=[shape((4 * rows, model), BF16), s...  59.6 us
    dot_general x6, matrix products, dot(): return lax.dot_general(a, b, (dims, ((), ())), preferred_element_type=F32)  31.8 us

profile of v4, /device:TPU:0, one launch (start us, length us, event | category | flops | bytes accessed | tf_op | source)
XLA Modules:
  0.0 278.8 jit_solution(2313885852038656185)
XLA Ops:
  0.6 0.0 copy-start.5
  1.5 0.9 dynamic-slice_reduce_fusion
  2.4 0.6 reshape.86.refs_2_.refs_5_
  3.0 0.6 reshape.87.refs_3_
  4.2 0.7 fusion.7
  4.9 1.2 broadcast_in_dim.14.refs_9_.refs_13_
  6.1 59.6 %front.1 = (bf16[1024,1024]{1,0:T(8,128)(2,1)}, bf16[1024,1024]{1,0:T(8,128)(2,1)}, bf16[1024,256]{1,0:T(8,128)(2,1)}, bf16[1024,256]{1,0:T(8,128)(2,1)}, bf16[2...) custom-call(bf16[256,1024]{1,0:T(8,128)(2,1)} %refs_3_.1, ...), custom_call_target="tpu_custom_call" | custom-call | tf_op jit(solution)/shard_map/front/pallas_call | solution.py:761
  65.7 0.0 copy-done.5
  65.7 0.0 copy-start.3
  65.7 0.0 copy-start.4
  65.7 0.0 copy-start.7
  65.8 4.1 %fusion.10 = f32[1024,1024]{1,0:T(8,128)S(1)} fusion(bf16[1024,1024]{1,0:T(8,128)(2,1)} %get-tuple-element.31, bf16[1024,1024]{1,0:T(8,128)(2,1)S(1)} %copy-done.5), kind=kOutput, calls=%fused_computation.40 | convolution fusion | flops 2147483648 | bytes 8388608 | tf_op jit(solution)/shard_map/dot_general | solution.py:799
  69.8 0.0 copy-done.3
  69.8 0.0 copy-done.4
  69.8 0.0 copy-done.7
  69.9 12.8 %convert_reduce_fusion = (f32[1024]{0:T(1024)}, bf16[1024,1024]{1,0:T(8,128)(2,1)S(1)}, f32[1024,1024]{1,0:T(8,128)S(1)}) fusion(f32[1024,1024]{1,0:T(8,128)S(1)} %fusion.10, f32[1024]{0:T(1024)S(1)} %copy-done.3, bf16[1024,1024]{1,0:T(8,128)(2,1)S(1)} %copy-done.7, bf16[1024,1024]{1,0:T(8,128)(2,1)S(1)} %copy-done.4), kind=kOutput, calls=%fused_computation.2 | convolution fusion | flops 2226125824 | bytes 14688256 | tf_op jit(solution)/shard_map/dot_general | solution.py:799
  82.7 1.1 multiply_convert_fusion
  83.8 3.7 %convolution_convert_fusion.refs_20_ = bf16[1024,1024]{1,0:T(8,128)(2,1)} fusion(bf16[1024,1024]{1,0:T(8,128)(2,1)S(1)} %multiply_convert_fusion, bf16[1024,1024]{1,0:T(8,128)(2,1)S(1)} %copy-done.7), kind=kOutput, calls=%fused_computation.18 | convolution fusion | flops 2148532224 | bytes 6291456 | tf_op jit(solution)/shard_map/dot_general | solution.py:799
  87.6 0.0 copy-start.6
  87.6 3.7 %convolution_convert_fusion.2.refs_1_ = bf16[1024,1024]{1,0:T(8,128)(2,1)} fusion(bf16[1024,1024]{1,0:T(8,128)(2,1)S(1)} %multiply_convert_fusion, bf16[1024,1024]{1,0:T(8,128)(2,1)S(1)} %copy-done.4), kind=kOutput, calls=%fused_computation.20 | convolution fusion | flops 2148532224 | bytes 6291456 | tf_op jit(solution)/shard_map/dot_general | solution.py:799
  91.3 0.0 copy-done.6
  91.3 3.8 %convolution_convert_fusion.1.refs_19_ = bf16[1024,1024]{1,0:T(8,128)(2,1)} fusion(bf16[1024,1024]{1,0:T(8,128)(2,1)S(1)} %copy-done.6, bf16[1024,1024]{1,0:T(8,128)(2,1)S(1)} %get-tuple-element.63), kind=kOutput, calls=%fused_computation.19 | convolution fusion | flops 2148532224 | bytes 6291456 | tf_op jit(solution)/shard_map/dot_general | solution.py:799
  95.0 3.7 %convolution_convert_fusion.3.refs_0_ = bf16[1024,1024]{1,0:T(8,128)(2,1)} fusion(bf16[1024,1024]{1,0:T(8,128)(2,1)S(1)} %get-tuple-element.63, bf16[1024,1024]{1,0:T(8,128)(2,1)S(1)} %copy-done.5), kind=kOutput, calls=%fused_computation.21 | convolution fusion | flops 2148532224 | bytes 6291456 | tf_op jit(solution)/shard_map/dot_general | solution.py:799
  98.7 0.7 broadcast_in_dim.26.refs_22_
  99.4 162.5 %late.1 = (bf16[256,1024]{1,0:T(8,128)(2,1)}, f32[256,1024]{1,0:T(8,128)}, bf16[1024,1024]{1,0:T(8,128)(2,1)}, bf16[1024,1024]{1,0:T(8,128)(2,1)}, bf16[1024,1024]{1,0:T(8,128)(2,1)}, /*index=5*/bf16[256,128]{1,0:T(8,128)(2,1)}) custom-call(bf16[1024,1024]{1,0:T(8,128)(2,1)} %convolution_convert_fusion.3.refs_0_, ...), custom_call_target="tpu_custom_call" | custom-call | tf_op jit(solution)/shard_map/late/pallas_call | solution.py:633
  261.9 3.3 %convert_bitcast_fusion = (f32[256,1024]{0,1:T(8,128)S(1)}, f32[1024,256]{1,0:T(8,128)}, f32[1024,256]{1,0:T(8,128)}, f32[1024,256]{1,0:T(8,128)}) fusion(bf16[1024,1024]{1,0:T(8,128)(2,1)} %get-tuple-element.44), kind=kLoop, calls=%fused_computation.22 | loop fusion | flops 1048576 | bytes 6291456 | tf_op jit(solution)/shard_map/convert_element_type | solution.py:904
  265.2 0.0 copy-start
  265.2 1.3 copy.35
  266.5 4.1 %convert_element_type.66 = f32[1024,1024]{1,0:T(8,128)} convert(bf16[1024,1024]{1,0:T(8,128)(2,1)} %get-tuple-element.45) | non-fusion elementwise | flops 1048576 | bytes 6291456 | tf_op jit(solution)/shard_map/convert_element_type | solution.py:906
  270.6 0.0 copy-start.2
  270.6 0.0 copy-done
  270.6 0.0 copy-start.1
  270.6 2.5 convert_element_type.67
  273.1 0.0 copy-done.2
  273.1 0.1 reshape.93
  273.2 0.1 fusion.9
  273.2 0.7 copy.40
  273.9 0.7 copy.41
  274.6 0.6 slice_bitcast_fusion
  275.2 0.6 slice_bitcast_fusion.3
  275.7 1.9 copy.46
  277.6 0.0 copy-done.1
  277.6 1.0 copy.47
  (3 shorter events, 0.0 us)
Async XLA Ops:
  0.6 65.1 %copy-start.5 = (bf16[1024,1024]{1,0:T(8,128)(2,1)S(1)}, bf16[1024,1024]{1,0:T(8,128)(2,1)}, u32[]{:S(2)}) copy-start(bf16[1024,1024]{1,0:T(8,128)(2,1)} %param.29) | copy-start | bytes 6291460
  65.7 4.1 %copy-start.3 = (f32[1024]{0:T(1024)S(1)}, f32[1024]{0:T(1024)}, u32[]{:S(2)}) copy-start(f32[1024]{0:T(1024)} %param.30) | copy-start | bytes 12292
  65.7 4.1 %copy-start.4 = (bf16[1024,1024]{1,0:T(8,128)(2,1)S(1)}, bf16[1024,1024]{1,0:T(8,128)(2,1)}, u32[]{:S(2)}) copy-start(bf16[1024,1024]{1,0:T(8,128)(2,1)} %param.31) | copy-start | bytes 6291460
  65.7 4.1 %copy-start.7 = (bf16[1024,1024]{1,0:T(8,128)(2,1)S(1)}, bf16[1024,1024]{1,0:T(8,128)(2,1)}, u32[]{:S(2)}) copy-start(bf16[1024,1024]{1,0:T(8,128)(2,1)} %get-tuple-element.32) | copy-start | bytes 6291460
  87.6 3.7 %copy-start.6 = (bf16[1024,1024]{1,0:T(8,128)(2,1)S(1)}, bf16[1024,1024]{1,0:T(8,128)(2,1)}, u32[]{:S(2)}) copy-start(bf16[1024,1024]{1,0:T(8,128)(2,1)} %get-tuple-element.31) | copy-start | bytes 6291460
  265.2 5.4 %copy-start = (bf16[1024,1024]{1,0:T(8,128)(2,1)S(1)}, bf16[1024,1024]{1,0:T(8,128)(2,1)}, u32[]{:S(2)}) copy-start(bf16[1024,1024]{1,0:T(8,128)(2,1)} %get-tuple-element.46) | copy-start | bytes 6291460
  270.6 2.5 copy-start.2
  270.6 7.0 %copy-start.1 = (f32[256,1024]{1,0:T(8,128)S(1)}, f32[256,1024]{1,0:T(8,128)}, u32[]{:S(2)}) copy-start(f32[256,1024]{1,0:T(8,128)} %get-tuple-element.94) | copy-start | bytes 3145732
